TPU v7x, 512 devices: a whole 4x4x16 slice. The times are simulated.
512 devices in a mesh: dp: 64 (over z_lo, x, core), ens: 8 (over y, z_hi).
Axes of the slice: x: 4, y: 4, z: 16 (z_hi: 2, z_lo: 8; z = z_hi * 8 + z_lo), core: 2. Of those that a mesh axis runs over, the one named last changes fastest.
Arguments:
- embeddings: bfloat16 [49152, 1024], P('dp'), may hold values from -6 to 6
- valid_mask: int32 [49152], P('dp'), may hold values 0 or 1
- first_weight: bfloat16 [8, 1024, 4096], P(None, 'dp', 'ens'), may hold values from -0.1875 to 0.1875
- second_weight: bfloat16 [8, 4096, 128], P(None, 'ens'), may hold values from -0.09375 to 0.09375
- thresholds: int32 [8], replicated, may hold values from -256 to 256
Outputs:
- mean_logits: float32 [49152, 128], P('dp')
- kept_share: float32 [8], P('ens')
- agree_share: float32 [8], P('ens')
All inputs are finite; a program needn't handle non-finite values. No bound on the sum of `valid_mask` on one device may be relied on, other than what follows from the above.
Results may differ from a plain program's by a relative error of at most 0.0044.
Values may be sent and summed in bfloat16 or wider, within the bound.
No kernel may reach another device: no remote copies, remote signals or barrier semaphores. Data moves between devices by JAX's collectives and lax.ppermute only.
A program may use at most 64 MiB of HBM per device.

v0:
```python
import jax
import jax.numpy as jnp
from jax import lax
from jax.sharding import PartitionSpec as P


def split_up(shard, dim, size):
    shape = shard.shape
    blocks = shard.reshape(*shape[:dim], size, shape[dim] // size, *shape[dim + 1 :])
    return jnp.moveaxis(blocks, dim, 0)


def cut_rows(length, count):
    lap = length // count
    if lap >= 8:
        lap -= lap % 8
    return [lap * k for k in range(1, count)]


def in_order(blocks, dim):
    shape = list(blocks.shape[1:])
    shape[dim] *= blocks.shape[0]
    return jnp.moveaxis(blocks, 0, dim).reshape(shape)


def several_exchanges(shard, axis, pieces, split_dim, concat_dim):
    blocks = split_up(shard, split_dim, lax.axis_size(axis))
    split_at = max(range(1, max(2, blocks.ndim - 1)), key=lambda d: blocks.shape[d])
    done = []
    for section in jnp.split(blocks, cut_rows(blocks.shape[split_at], pieces), axis=split_at):
        if section.size:
            done.append(lax.all_to_all(section, axis, split_axis=0, concat_axis=0, tiled=True))
    return in_order(jnp.concatenate(done, axis=split_at), concat_dim)


def from_everyone(shard, axis):
    copies = jnp.broadcast_to(shard, (lax.axis_size(axis), *shard.shape))
    return lax.all_to_all(copies, axis, split_axis=0, concat_axis=0, tiled=True)


def over_copies(shard, axis):
    everything = from_everyone(shard, axis)
    return jnp.sum(everything.astype(jnp.float32), axis=0)


def of_everyone(shard, axis):
    return from_everyone(shard, axis).sum(axis=0)


def in_one(arrays, axis):
    ends = [0]
    for a in arrays:
        ends.append(ends[-1] + a.size)
    total = of_everyone(jnp.concatenate([a.ravel() for a in arrays]), axis)
    return tuple((total[b:e].reshape(a.shape) for a, b, e in zip(arrays, ends, ends[1:])))


def on_device(embeddings, valid_mask, first_weight, second_weight, thresholds):
    member = lax.axis_index("ens")
    own_first = lax.all_to_all(first_weight, "ens", split_axis=0, concat_axis=2, tiled=True)
    own_second = several_exchanges(second_weight, "ens", 2, 0, 1)
    full_first = lax.all_gather(own_first[0], "dp", axis=0, tiled=True)
    hidden = jnp.maximum(
        jnp.dot(embeddings, full_first, preferred_element_type=jnp.float32), 0.0
    ).astype(jnp.bfloat16)
    logits_own = jnp.dot(hidden, own_second[0], preferred_element_type=jnp.float32)
    classes = logits_own.shape[1]
    levels = jnp.arange(classes, dtype=jnp.float32)
    grades = (2.0 * levels / (classes - 1) - 1.0) * jnp.sqrt(jnp.float32(3.0 / classes))
    scores = jnp.dot(logits_own, grades, precision=lax.Precision.HIGHEST)
    cutoffs = thresholds.astype(jnp.float32) / 256.0
    own_cutoff = lax.dynamic_index_in_dim(cutoffs, member, 0, keepdims=False)
    validity = valid_mask.astype(jnp.float32)
    kept_soft = validity * jax.nn.sigmoid(4.0 * (scores - own_cutoff))
    mean_logits = (
        over_copies(logits_own.astype(jnp.bfloat16), "ens").astype(jnp.float32)
        / first_weight.shape[0]
    )
    ens_score = jnp.dot(mean_logits, grades, precision=lax.Precision.HIGHEST)
    ens_kept = jax.nn.sigmoid(4.0 * (ens_score - jnp.mean(cutoffs)))
    agree_local = jnp.sum(kept_soft * ens_kept)
    kept_total, agree_total = in_one((jnp.sum(kept_soft), agree_local), "dp")
    shard_docs = embeddings.shape[0]
    return (
        mean_logits,
        (kept_total / shard_docs).reshape(1),
        (agree_total / shard_docs).reshape(1),
    )


def solution(mesh):
    return jax.shard_map(
        on_device,
        mesh=mesh,
        in_specs=(P("dp", None), P("dp"), P(None, "dp", "ens"), P(None, "ens", None), P()),
        out_specs=(P("dp", None), P("ens"), P("ens")),
        check_vma=False,
    )
```

profile of v0, /device:TPU:1, one launch (start us, length us, event | category | flops | bytes accessed | tf_op | source)
XLA Modules:
  0.0 333.6 jit_solution(111445874965293776)
XLA Ops:
  7.2 0.0 copy-start
  7.2 0.0 all-gather.2.cloned.1.call-start
  7.2 32.7 %all_to_all.36 = bf16[8,16,512]{2,1,0:T(8,128)(2,1)S(1)} all-to-all(bf16[8,16,512]{2,1,0:T(8,128)(2,1)} %param.7), channel_id=1, replica_groups=mesh['dp'=64,'ens'=8] {'ens'}, dimensions={0} | all-to-all | bytes 262144 | tf_op jit(solution)/shard_map/all_to_all | solution.py:60
  39.9 0.7 copy.16
  40.5 0.0 all-gather.2.cloned.1.call-update
  40.6 1.3 fusion.12
  41.9 19.8 %all_to_all.37 = bf16[8,1,256,128]{3,2,1,0:T(8,128)(2,1)S(1)} all-to-all(bf16[8,1,256,128]{3,2,1,0:T(8,128)(2,1)S(1)} %get-tuple-element.6), channel_id=1, replica_groups=mesh['dp'=64,'ens'=8] {'ens'}, dimensions={0} | all-to-all | bytes 1048576 | tf_op jit(solution)/shard_map/all_to_all | solution.py:32
  61.7 27.5 %all_to_all.38 = bf16[8,1,256,128]{3,2,1,0:T(8,128)(2,1)S(1)} all-to-all(bf16[8,1,256,128]{3,2,1,0:T(8,128)(2,1)S(1)} %get-tuple-element.5), channel_id=1, replica_groups=mesh['dp'=64,'ens'=8] {'ens'}, dimensions={0} | all-to-all | bytes 1048576 | tf_op jit(solution)/shard_map/all_to_all | solution.py:32
  89.2 0.1 pad_maximum_fusion
  89.3 104.5 %all-gather.2.cloned.1.call-done = bf16[1024,4096]{1,0:T(8,128)(2,1)} async-done(((bf16[16,4096]{1,0:T(8,128)(2,1)}), bf16[1024,4096]{1,0:T(8,128)(2,1)}) %all-gather.2.cloned.1.call-update) | async-done | bytes 8388624 | tf_op jit(solution)/shard_map/all_gather | solution.py:62
  193.7 0.0 copy-done
  193.8 11.8 %fusion.14 = (bf16[768,128]{1,0:T(8,128)(2,1)S(1)}, f32[768,128]{1,0:T(8,128)S(1)}) fusion(bf16[4096,128]{1,0:T(8,128)(2,1)S(1)} %bitcast.25, bf16[768,1024]{1,0:T(8,128)(2,1)S(1)} %copy-done, bf16[1024,4096]{1,0:T(8,128)(2,1)} %all-gather.2.cloned.1.call-done), kind=kOutput, calls=%fused_computation.25 | convolution fusion | flops 7254147072 | bytes 11599872 | tf_op jit(solution)/shard_map/dot_general | solution.py:66
  205.5 0.0 copy-start.3
  205.6 1.4 broadcast_in_dim.6
  206.9 0.0 copy-start.2
  206.9 11.8 %all-to-all-start.3 = ((bf16[8,768,128]{2,1,0:T(8,128)(2,1)}), bf16[8,768,128]{2,1,0:T(8,128)(2,1)S(1)}, u32[]{:S(2)}, u32[]{:S(2)}) async-start(bf16[8,768,128]{2,1,0:T(8,128)(2,1)} %broadcast_in_dim.6), calls=%async_computation.3 | async-start | bytes 3145728 | tf_op jit(solution)/shard_map/all_to_all | solution.py:38
  218.7 0.0 copy-done.3
  218.7 0.6 fusion.10
  219.3 0.6 dynamic_slice.4
  220.5 0.5 convolution_reduce_fusion.1
  221.0 34.4 %all-to-all-done.3 = bf16[8,768,128]{2,1,0:T(8,128)(2,1)S(1)} async-done(((bf16[8,768,128]{2,1,0:T(8,128)(2,1)}), bf16[8,768,128]{2,1,0:T(8,128)(2,1)S(1)}, u32[]{:S(2)}, u32[]{:S(2)}) %all-to-all-start.3) | async-done | bytes 1572896 | tf_op jit(solution)/shard_map/all_to_all | solution.py:38
  255.4 0.2 convert_reduce_fusion
  255.7 0.0 copy-start.1
  255.7 0.5 convolution_reduce_fusion
  256.1 0.0 copy-done.2
  256.1 1.3 fusion.11
  257.5 1.4 pad_maximum_fusion.1
  258.9 63.6 %all_to_all.39 = f32[64,1,2]{2,1,0:T(1,128)S(1)} all-to-all(f32[64,1,2]{2,1,0:T(1,128)S(1)} %broadcast_in_dim.7), channel_id=1, replica_groups=mesh['dp'=64,'ens'=8] {'dp'}, dimensions={0} | all-to-all | bytes 1024 | tf_op jit(solution)/shard_map/all_to_all | solution.py:38
  322.5 0.1 reduce_sum.49
  322.6 0.6 fusion.13
  324.5 0.0 copy-done.1
  (2 shorter events, 0.1 us)
Async XLA Ops:
  7.2 186.6 %copy-start = (bf16[768,1024]{1,0:T(8,128)(2,1)S(1)}, bf16[768,1024]{1,0:T(8,128)(2,1)}, u32[]{:S(2)}) copy-start(bf16[768,1024]{1,0:T(8,128)(2,1)} %param.5) | copy-start | bytes 4718596
  7.2 186.6 %all-gather.2.cloned.1.call-start = ((), (), s32[]{:S(2)}) async-start(), calls=%async_computation.5 | async-start | bytes 8519680 | tf_op jit(solution)/shard_map/all_gather | solution.py:62
  205.5 13.1 %copy-start.3 = (s32[8]{0:T(128)S(1)}, s32[8]{0:T(128)}, u32[]{:S(2)}) copy-start(s32[8]{0:T(128)} %param.9) | copy-start | bytes 100
  206.9 49.2 %copy-start.2 = (s32[768]{0:T(1024)S(1)}, s32[768]{0:T(1024)}, u32[]{:S(2)}) copy-start(s32[768]{0:T(1024)} %param.6) | copy-start | bytes 9220
  206.9 48.5 %all-to-all-start.3 = ((bf16[8,768,128]{2,1,0:T(8,128)(2,1)}), bf16[8,768,128]{2,1,0:T(8,128)(2,1)S(1)}, u32[]{:S(2)}, u32[]{:S(2)}) async-start(bf16[8,768,128]{2,1,0:T(8,128)(2,1)} %broadcast_in_dim.6), calls=%async_computation.3 | async-start | bytes 3145728 | tf_op jit(solution)/shard_map/all_to_all | solution.py:38
  255.7 68.9 %copy-start.1 = (f32[768,128]{1,0:T(8,128)}, f32[768,128]{1,0:T(8,128)S(1)}, u32[]{:S(2)}) copy-start(f32[768,128]{1,0:T(8,128)S(1)} %broadcast_multiply_fusion) | copy-start | bytes 1179652
Sparse Core Ops, SparseCore 0:
  40.7 153.0 all-gather.1
where the time goes:
time: 334 us
  blocking collectives  144 us (43%)
  waiting for transfers between devices  139 us (42%)
  between operations  18.3 us (5%)
  matrix products  12.7 us (4%)
  starting transfers between devices  11.8 us (4%)
  local copies, waits for them, and re-layouts  4.51 us (1%)
  other arithmetic  3.76 us (1%)
    all_gather x1, waiting for transfers between devices, on_device(): full_first = lax.all_gather(own_first[0], 'dp', axis=0, tiled=True)  104 us
    all_to_all x1, blocking collectives, from_everyone(): return lax.all_to_all(copies, axis, split_axis=0, concat_axis=0, tiled=True)  63.6 us
    all_to_all x2, blocking collectives, several_exchanges(): lax.all_to_all(section, axis, split_axis=0, concat_axis=0, tiled=True)  47.4 us
    all_to_all x1, waiting for transfers between devices, from_everyone(): return lax.all_to_all(copies, axis, split_axis=0, concat_axis=0, tiled=True)  34.4 us
    all_to_all x1, blocking collectives, on_device(): lax.all_to_all(first_weight, 'ens', split_axis=0, concat_axis=2, tiled=True)  32.7 us
    dot_general x1, matrix products, on_device(): jnp.dot(hidden, own_second[0], preferred_element_type=jnp.float32)  11.8 us
    all_to_all x1, starting transfers between devices, from_everyone(): return lax.all_to_all(copies, axis, split_axis=0, concat_axis=0, tiled=True)  11.8 us
  transfers between devices with their start and end apart: 2, of which 2 were waited for; matrix products, arithmetic and copies ran while one was open for 1% of the time, Pallas kernels for 0%

commit v1 on v0

v1 whole, which is shorter than its diff:
```python
import functools

import jax
import jax.numpy as jnp
import ml_dtypes
import numpy as np
from jax import lax
from jax.experimental import pallas as pl
from jax.experimental.pallas import tpu as pltpu
from jax.sharding import Mesh, PartitionSpec as P

F32 = jnp.float32
BF16 = jnp.bfloat16
LANES = 128


def exchange(blocks, axes):
    return lax.all_to_all(blocks, axes, split_axis=0, concat_axis=0, tiled=True)


def to_all(block, axes):
    return exchange(jnp.broadcast_to(block, (lax.axis_size(axes), *block.shape)), axes)


def swap(array, axis):
    return lax.ppermute(array, axis, [(0, 1), (1, 0)])


def grade_parts(classes):
    levels = np.arange(classes, dtype=np.float32)
    rest = (np.float32(2.0) * levels / np.float32(classes - 1) - np.float32(1.0)) * np.sqrt(np.float32(3.0 / classes))
    parts = np.zeros((classes, LANES), np.float32)
    for k in range(3):
        part = rest.astype(ml_dtypes.bfloat16).astype(np.float32)
        parts[:, k] = part
        rest = rest - part
    return parts.astype(ml_dtypes.bfloat16)


def score_kernel(core_ref, docs_ref, own_ref, other_ref, second_ref, grades_ref, mean_ref, scores_ref, first, total, marks):
    member = pl.program_id(0)
    n_x, n_z = own_ref.shape[0], own_ref.shape[1]
    core = core_ref[0]
    for x in range(n_x):
        for z in range(n_z):
            first[z, x, core] = own_ref[x, z, 0]
            first[z, x, 1 - core] = other_ref[x, z, 0]
    width = first.shape[-1]
    weight = first[...].reshape(docs_ref.shape[1], width)
    hidden = jnp.maximum(jnp.dot(docs_ref[...], weight, preferred_element_type=F32), 0.0).astype(BF16)
    second = second_ref[0]
    direction = jnp.sum(jnp.dot(second, grades_ref[...], preferred_element_type=F32), axis=1, keepdims=True)
    high = direction.astype(BF16)
    low = (direction - high.astype(F32)).astype(BF16)
    lane = lax.broadcasted_iota(jnp.int32, (width, LANES), 1)
    zero = jnp.zeros((width, LANES), F32)
    along = jnp.where(lane == 2 * member, high.astype(F32), jnp.where(lane == 2 * member + 1, low.astype(F32), zero)).astype(BF16)
    both = jnp.concatenate([second, along], axis=1)
    part = jnp.dot(hidden, both, preferred_element_type=F32)

    @pl.when(member == 0)
    def _():
        total[...] = part

    @pl.when(member > 0)
    def _():
        total[...] += part

    @pl.when(member == pl.num_programs(0) - 1)
    def _():
        mean_ref[...] = total[:, :LANES].astype(BF16)
        scores_ref[...] = lax.dot_general(
            marks[...], total[:, LANES:], (((1,), (1,)), ((), ())),
            precision=lax.Precision.HIGHEST, preferred_element_type=F32,
        )

    @pl.when(member == 0)
    def _():
        row = lax.broadcasted_iota(jnp.int32, marks.shape, 0)
        col = lax.broadcasted_iota(jnp.int32, marks.shape, 1)
        marks[...] = jnp.where(col // 2 == row, 1.0, 0.0).astype(F32)


def score(core, docs, own, other, second, grades):
    n_x, n_z, members, rows, width = own.shape
    n_docs, depth = docs.shape
    block = (n_x, n_z, 1, rows, width)
    whole = lambda m, c: (0, 0)
    piece = lambda m, c: (0, 0, m, 0, 0)
    return pl.pallas_call(
        score_kernel,
        grid_spec=pltpu.PrefetchScalarGridSpec(
            num_scalar_prefetch=1,
            grid=(members,),
            in_specs=[
                pl.BlockSpec((n_docs, depth), whole),
                pl.BlockSpec(block, piece),
                pl.BlockSpec(block, piece),
                pl.BlockSpec((1, width, LANES), lambda m, c: (m, 0, 0)),
                pl.BlockSpec((LANES, LANES), whole),
            ],
            out_specs=[pl.BlockSpec((n_docs, LANES), whole), pl.BlockSpec((8, n_docs), whole)],
            scratch_shapes=[
                pltpu.VMEM((n_z, n_x, 2, rows, width), BF16),
                pltpu.VMEM((n_docs, 2 * LANES), F32),
                pltpu.VMEM((8, LANES), F32),
            ],
        ),
        out_shape=[jax.ShapeDtypeStruct((n_docs, LANES), BF16), jax.ShapeDtypeStruct((8, n_docs), F32)],
        compiler_params=pltpu.CompilerParams(dimension_semantics=("arbitrary",), vmem_limit_bytes=40 * 1024 * 1024),
    )(core, docs, own, other, second, grades)


def halves(scores):
    high = lax.reduce_precision(scores, 8, 7)
    low = lax.reduce_precision(scores - high, 8, 7)
    return jnp.stack([high, low]).astype(BF16)


def on_device(embeddings, valid_mask, first_weight, second_weight, thresholds):
    members, rows, width = first_weight.shape
    n_docs = embeddings.shape[0]
    half = members // 2
    z_axes = ("za", "zp")
    n_za, n_x, n_y = lax.axis_size("za"), lax.axis_size("x"), lax.axis_size("y")
    parity = lax.axis_index("zp")
    core = lax.axis_index("core").reshape(1).astype(jnp.int32)

    blocks = first_weight.reshape(1, 2, half, rows, width)
    blocks = jnp.broadcast_to(blocks, (n_za, *blocks.shape[1:])).reshape(n_za * 2, half, rows, width)
    along_z = exchange(blocks, z_axes)
    docs, along_z = lax.optimization_barrier((embeddings, along_z))
    docs_near = swap(docs, "zp")
    own = to_all(along_z, "x")
    other = swap(own, "core")
    second = lax.dynamic_slice_in_dim(second_weight, parity * half, half, 0)
    grades = jnp.asarray(grade_parts(second_weight.shape[2]))
    mean_own, scores_own = score(core, docs, own, other, second, grades)
    mean_near, scores_near = score(core, docs_near, own, other, second, grades)

    quarter = n_docs // n_y
    score_rows = half * n_docs // LANES

    def packed(mean, scores):
        parts = halves(scores[:half]).reshape(1, 2 * score_rows, LANES)
        parts = jnp.broadcast_to(parts, (n_y, *parts.shape[1:]))
        return jnp.concatenate([mean.reshape(n_y, quarter, LANES), parts], axis=1)

    mine, near = packed(mean_own, scores_own), packed(mean_near, scores_near)
    even = parity == 0
    blocks = jnp.concatenate([jnp.where(even, mine, near), jnp.where(even, near, mine)], axis=0)
    blocks = exchange(blocks, ("zp", "y"))
    part_mean = lax.reduce_precision(jnp.sum(blocks[:, :quarter].astype(F32), axis=0), 8, 7).astype(BF16)
    part_scores = blocks[:, quarter:].astype(F32).reshape(2, n_y * 2, score_rows, LANES).sum(axis=1)
    packed_scores = halves(part_scores.reshape(2 * score_rows, LANES)).reshape(4 * score_rows, LANES)
    message = jnp.concatenate([part_mean, packed_scores], axis=0)
    answer = swap(message, "zh")
    both = message.astype(F32) + answer.astype(F32)
    mean_quarter = (both[:quarter] * (1.0 / members)).astype(BF16)
    mean_logits = to_all(mean_quarter, "y").reshape(n_docs, LANES).astype(F32)
    scores = (both[quarter : quarter + 2 * score_rows] + both[quarter + 2 * score_rows :]).reshape(members, n_docs)

    cutoffs = thresholds.astype(F32) / 256.0
    validity = valid_mask.astype(F32)
    kept_soft = validity[None, :] * jax.nn.sigmoid(4.0 * (scores - cutoffs[:, None]))
    ens_score = jnp.sum(scores, axis=0) / members
    ens_kept = jax.nn.sigmoid(4.0 * (ens_score - jnp.mean(cutoffs)))
    counts = jnp.stack([jnp.sum(kept_soft, axis=1), jnp.sum(kept_soft * ens_kept[None, :], axis=1)])
    counts = to_all(counts, ("x", "core")).sum(axis=0)
    counts = to_all(counts, z_axes).sum(axis=0)
    member = lax.axis_index("y") * 2 + lax.axis_index("zh")
    shares = lax.dynamic_slice_in_dim(counts, member, 1, 1) / n_docs
    return mean_logits, shares[0], shares[1]


def solution(mesh):
    devices = mesh.devices.reshape(4, 2, 4, 2, 4, 2)
    fine = Mesh(devices, ("za", "zp", "x", "core", "y", "zh"))
    dp, ens = ("za", "zp", "x", "core"), ("y", "zh")
    return jax.shard_map(
        on_device,
        mesh=fine,
        in_specs=(P(dp, None), P(dp), P(None, dp, ens), P(None, ens, None), P()),
        out_specs=(P(dp, None), P(ens), P(ens)),
        check_vma=False,
    )
```

time: 334 us -> 206 us (0.62)
  blocking collectives: 144 us -> 58.5 us
  waiting for transfers between devices: 139 us -> 65.3 us
  starting transfers between devices: 11.8 us -> 50 us
  Pallas kernels: 0 us -> 19.8 us
  between operations: 18.3 us -> 1.6 us
  matrix products: 12.7 us -> 0 us
    all_gather x1 -> x0, waiting for transfers between devices: 104 us -> none  [on_device(): full_first = lax.all_gather(own_first[0], 'dp', axis=0, tiled=True)]
    all_to_all x4 -> x2, blocking collectives: 144 us -> 58.5 us  [exchange(): return lax.all_to_all(blocks, axes, split_axis=0, concat_axis=0, tiled=True)]
    ppermute x0 -> x3, waiting for transfers between devices: none -> 39.4 us  [swap(): return lax.ppermute(array, axis, [(0, 1), (1, 0)])]
    ppermute x0 -> x3, starting transfers between devices: none -> 24.7 us  [swap(): return lax.ppermute(array, axis, [(0, 1), (1, 0)])]
    pallas_call x0 -> x2, Pallas kernels: none -> 19.8 us  [score(): pl.pallas_call(score_kernel, grid_spec=pltpu.PrefetchScalarGridSpec(num_s...]
    all_to_all x1 -> x4, starting transfers between devices: 11.8 us -> 25.3 us  [exchange(): return lax.all_to_all(blocks, axes, split_axis=0, concat_axis=0, tiled=True)]
    dot_general x3 -> x0, matrix products: 12.7 us -> none  [the longest x1 11.8 us: on_device(): jnp.dot(hidden, own_second[0], preferred_element_type=jnp.float32)]
    all_to_all x1 -> x4, waiting for transfers between devices: 34.4 us -> 25.9 us  [exchange(): return lax.all_to_all(blocks, axes, split_axis=0, concat_axis=0, tiled=True)]
  transfers between devices with their start and end apart: 2 -> 7, of which waited for: 2 -> 6; matrix products, arithmetic and copies ran while one was open for 1% -> 1% of each run, Pallas kernels for 0% -> 0%
where the time goes in v1:
time: 206 us; the launch traced here: 204 us
  waiting for transfers between devices  65.3 us (32%)
  blocking collectives  58.5 us (28%)
  starting transfers between devices  50 us (24%)
  Pallas kernels  19.8 us (10%)
  local copies, waits for them, and re-layouts  5.98 us (3%)
  other arithmetic  3.13 us (2%)
    all_to_all x2, blocking collectives, exchange(): return lax.all_to_all(blocks, axes, split_axis=0, concat_axis=0, tiled=True)  58.5 us
    ppermute x3, waiting for transfers between devices, swap(): return lax.ppermute(array, axis, [(0, 1), (1, 0)])  39.4 us
    all_to_all x4, waiting for transfers between devices, exchange(): return lax.all_to_all(blocks, axes, split_axis=0, concat_axis=0, tiled=True)  25.9 us
    all_to_all x4, starting transfers between devices, exchange(): return lax.all_to_all(blocks, axes, split_axis=0, concat_axis=0, tiled=True)  25.3 us
    ppermute x3, starting transfers between devices, swap(): return lax.ppermute(array, axis, [(0, 1), (1, 0)])  24.7 us
    pallas_call x2, Pallas kernels, score(): pl.pallas_call(score_kernel, grid_spec=pltpu.PrefetchScalarGridSpec(num_s...  19.8 us
  transfers between devices with their start and end apart: 7, of which 6 were waited for; matrix products, arithmetic and copies ran while one was open for 1% of the time, Pallas kernels for 0%

profile of v1, /device:TPU:1, one launch (start us, length us, event | category | flops | bytes accessed | tf_op | source)
XLA Modules:
  0.0 204.4 jit_solution(1997453691977678418)
XLA Ops:
  0.6 0.0 copy-start
  0.6 1.0 broadcast_in_dim.33
  1.7 35.6 %all_to_all.30 = bf16[8,4,16,512]{3,2,1,0:T(8,128)(2,1)S(1)} all-to-all(bf16[8,4,16,512]{3,2,1,0:T(8,128)(2,1)S(1)} %bitcast.33), channel_id=1, replica_groups=mesh['za'=4,'zp'=2,'x'=4,'core'=2,'y'=4,'zh'=2] {'za','zp'}, dimensions={0} | all-to-all | bytes 1048576 | tf_op jit(solution)/shard_map/all_to_all | solution.py:18
  37.3 0.3 broadcast_in_dim.34
  37.5 0.0 copy-start.3
  37.5 23.0 %all_to_all.31.own_ref = bf16[4,8,4,16,512]{4,3,2,1,0:T(8,128)(2,1)S(1)} all-to-all(bf16[4,8,4,16,512]{4,3,2,1,0:T(8,128)(2,1)S(1)} %broadcast_in_dim.34), channel_id=1, replica_groups=mesh['za'=4,'zp'=2,'x'=4,'core'=2,'y'=4,'zh'=2] {'x'}, dimensions={0} | all-to-all | bytes 4194304 | tf_op jit(solution)/shard_map/all_to_all | solution.py:18
  60.5 10.0 %collective-permute-start = (bf16[4,8,4,16,512]{4,3,2,1,0:T(8,128)(2,1)S(1)}, bf16[4,8,4,16,512]{4,3,2,1,0:T(8,128)(2,1)}, u32[]{:S(2)}, u32[]{:S(2)}) collective-permute-start(bf16[4,8,4,16,512]{4,3,2,1,0:T(8,128)(2,1)S(1)} %all_to_all.31.own_ref), channel_id=1, source_target_pairs={{0,8},{8,0},{1,9},{9,1},{2,10},{10,2},{3,11},{11,3},{4,12},{12,4},... | collective-permute-start | bytes 6291464 | tf_op jit(solution)/shard_map/ppermute | solution.py:26
  70.5 6.7 %collective-permute-start.1 = (bf16[768,1024]{1,0:T(8,128)(2,1)}, bf16[768,1024]{1,0:T(8,128)(2,1)}, u32[]{:S(2)}, u32[]{:S(2)}) collective-permute-start(bf16[768,1024]{1,0:T(8,128)(2,1)} %docs_ref), channel_id=1, source_target_pairs={{0,64},{64,0},{1,65},{65,1},{2,66},{66,2},{3,67},{67,3},{4,68},{68... | collective-permute-start | bytes 4718600 | tf_op jit(solution)/shard_map/ppermute | solution.py:26
  77.2 0.0 copy-done
  77.3 0.0 copy-start.1
  77.3 35.0 %collective-permute-done.1.docs_ref = bf16[768,1024]{1,0:T(8,128)(2,1)} collective-permute-done((bf16[768,1024]{1,0:T(8,128)(2,1)}, bf16[768,1024]{1,0:T(8,128)(2,1)}, u32[]{:S(2)}, u32[]{:S(2)}) %collective-permute-start.1) | collective-permute-done | bytes 1572896 | tf_op jit(solution)/shard_map/ppermute | solution.py:26
  112.3 0.0 collective-permute-done.other_ref
  112.3 0.0 copy-done.3
  112.3 9.9 %shard_map.86 = (bf16[768,128]{1,0:T(8,128)(2,1)S(1)}, f32[8,768]{1,0:T(8,128)S(1)}) custom-call(s32[1]{0:T(128)} %bitcast.core_ref, bf16[768,1024]{1,0:T(8,128)(2,1)} %collective-permute-done.1.docs_ref, bf16[4,8,4,16,512]{4,3,2,1,0:T(8,128)(2,1)S(1)} %all_to_all.31.own_ref, bf16[4,8,4,16,512]{4,3,2,1,0:T(8,128)(2,1)} %collective-permute-done.other_ref, ...), custom_call_target="tpu_custom_call" | custom-call | tf_op jit(solution)/shard_map/pallas_call | solution.py:90
  122.2 0.0 copy-done.1
  122.3 0.0 copy-start.2
  122.3 1.0 copy-done.2
  123.3 0.0 copy-start.4
  123.3 0.8 copy-done.4
  124.1 9.9 %shard_map.85 = (bf16[768,128]{1,0:T(8,128)(2,1)S(1)}, f32[8,768]{1,0:T(8,128)S(1)}) custom-call(s32[1]{0:T(128)} %bitcast.core_ref, bf16[768,1024]{1,0:T(8,128)(2,1)} %docs_ref, bf16[4,8,4,16,512]{4,3,2,1,0:T(8,128)(2,1)S(1)} %all_to_all.31.own_ref, bf16[4,8,4,16,512]{4,3,2,1,0:T(8,128)(2,1)} %collective-permute-done.other_ref, ...), custom_call_target="tpu_custom_call" | custom-call | tf_op jit(solution)/shard_map/pallas_call | solution.py:90
  134.0 0.0 copy-start.5
  134.1 0.0 copy-start.6
  134.1 0.1 broadcast_select_fusion.1
  134.2 0.8 pad_maximum_fusion
  135.1 5.1 %all-to-all-start.2 = ((bf16[8,240,128]{2,1,0:T(8,128)(2,1)}), bf16[8,240,128]{2,1,0:T(8,128)(2,1)S(1)}, u32[]{:S(2)}, u32[]{:S(2)}) async-start(bf16[8,240,128]{2,1,0:T(8,128)(2,1)} %pad_maximum_fusion), calls=%async_computation.2 | async-start | bytes 983040 | tf_op jit(solution)/shard_map/all_to_all | solution.py:18
  140.1 0.0 copy-done.5
  140.2 7.4 %all-to-all-done.2 = bf16[8,240,128]{2,1,0:T(8,128)(2,1)S(1)} async-done(((bf16[8,240,128]{2,1,0:T(8,128)(2,1)}), bf16[8,240,128]{2,1,0:T(8,128)(2,1)S(1)}, u32[]{:S(2)}, u32[]{:S(2)}) %all-to-all-start.2) | async-done | bytes 491552 | tf_op jit(solution)/shard_map/all_to_all | solution.py:18
  147.6 0.1 convert_reduce_fusion
  147.7 8.0 %collective-permute-start.2 = (bf16[288,128]{1,0:T(8,128)(2,1)S(1)}, bf16[288,128]{1,0:T(8,128)(2,1)S(1)}, u32[]{:S(2)}, u32[]{:S(2)}) collective-permute-start(bf16[288,128]{1,0:T(8,128)(2,1)S(1)} %pad_maximum_fusion.3), channel_id=1, source_target_pairs={{0,1},{1,0},{2,3},{3,2},{4,5},{5,4},{6,7},{7,6},{8,9},{9,8},{10,11... | collective-permute-start | bytes 221192 | tf_op jit(solution)/shard_map/ppermute | solution.py:26
  155.7 0.0 copy-done.6
  155.8 0.6 fusion.11
  156.4 0.1 sub.44
  156.4 0.1 sub.45
  157.2 4.4 %collective-permute-done.2 = bf16[288,128]{1,0:T(8,128)(2,1)S(1)} collective-permute-done((bf16[288,128]{1,0:T(8,128)(2,1)S(1)}, bf16[288,128]{1,0:T(8,128)(2,1)S(1)}, u32[]{:S(2)}, u32[]{:S(2)}) %collective-permute-start.2) | collective-permute-done | bytes 73760 | tf_op jit(solution)/shard_map/ppermute | solution.py:26
  161.6 0.1 divide_multiply_fusion
  161.8 0.1 fusion.12
  161.9 0.1 reduce_sum.94
  162.0 0.1 reduce_sum.95
  162.1 0.1 reduce_sum.89
  162.2 0.1 reduce_sum.90
  162.3 0.6 broadcast_in_dim.38
  162.9 9.3 %all-to-all-start.4 = ((f32[8,2,8]{2,1,0:T(2,128)}), f32[8,2,8]{2,1,0:T(2,128)S(1)}, u32[]{:S(2)}, u32[]{:S(2)}) async-start(f32[8,2,8]{2,1,0:T(2,128)} %broadcast_in_dim.38), calls=%async_computation.4 | async-start | bytes 16384 | tf_op jit(solution)/shard_map/all_to_all | solution.py:18
  172.2 4.6 %all-to-all-done.4 = f32[8,2,8]{2,1,0:T(2,128)S(1)} async-done(((f32[8,2,8]{2,1,0:T(2,128)}), f32[8,2,8]{2,1,0:T(2,128)S(1)}, u32[]{:S(2)}, u32[]{:S(2)}) %all-to-all-start.4) | async-done | bytes 544 | tf_op jit(solution)/shard_map/all_to_all | solution.py:18
  176.9 0.6 broadcast_in_dim.39
  177.5 6.6 %all-to-all-start.5 = ((f32[8,2,8]{2,1,0:T(2,128)}), f32[8,2,8]{2,1,0:T(2,128)S(1)}, u32[]{:S(2)}, u32[]{:S(2)}) async-start(f32[8,2,8]{2,1,0:T(2,128)} %broadcast_in_dim.39), calls=%async_computation.5 | async-start | bytes 16384 | tf_op jit(solution)/shard_map/all_to_all | solution.py:18
  184.1 9.3 %all-to-all-done.5 = f32[8,2,8]{2,1,0:T(2,128)S(1)} async-done(((f32[8,2,8]{2,1,0:T(2,128)}), f32[8,2,8]{2,1,0:T(2,128)S(1)}, u32[]{:S(2)}, u32[]{:S(2)}) %all-to-all-start.5) | async-done | bytes 544 | tf_op jit(solution)/shard_map/all_to_all | solution.py:18
  193.4 0.7 broadcast_in_dim.37
  194.1 4.3 %all-to-all-start.3 = ((bf16[4,192,128]{2,1,0:T(8,128)(2,1)}), bf16[4,192,128]{2,1,0:T(8,128)(2,1)S(1)}, u32[]{:S(2)}, u32[]{:S(2)}) async-start(bf16[4,192,128]{2,1,0:T(8,128)(2,1)} %broadcast_in_dim.37), calls=%async_computation.3 | async-start | bytes 393216 | tf_op jit(solution)/shard_map/all_to_all | solution.py:18
  198.4 0.1 dynamic-slice_multiply_fusion
  198.5 0.5 fusion.13
  199.0 4.6 %all-to-all-done.3 = bf16[4,192,128]{2,1,0:T(8,128)(2,1)S(1)} async-done(((bf16[4,192,128]{2,1,0:T(8,128)(2,1)}), bf16[4,192,128]{2,1,0:T(8,128)(2,1)S(1)}, u32[]{:S(2)}, u32[]{:S(2)}) %all-to-all-start.3) | async-done | bytes 196640 | tf_op jit(solution)/shard_map/all_to_all | solution.py:18
  203.6 0.8 bitcast_convert_fusion
  (28 shorter events, 0.4 us)
Async XLA Ops:
  0.6 76.6 %copy-start = (bf16[8,512,128]{2,1,0:T(8,128)(2,1)S(1)}, bf16[8,512,128]{2,1,0:T(8,128)(2,1)}, u32[]{:S(2)}) copy-start(bf16[8,512,128]{2,1,0:T(8,128)(2,1)} %param.9) | copy-start | bytes 3145732
  37.5 74.8 %copy-start.3 = (bf16[128,128]{1,0:T(8,128)(2,1)S(1)}, bf16[128,128]{1,0:T(8,128)(2,1)}, u32[]{:S(2)}) copy-start(bf16[128,128]{1,0:T(8,128)(2,1)} %constant.45.clone.grades_ref) | copy-start | bytes 98308
  60.5 51.8 %collective-permute-start = (bf16[4,8,4,16,512]{4,3,2,1,0:T(8,128)(2,1)S(1)}, bf16[4,8,4,16,512]{4,3,2,1,0:T(8,128)(2,1)}, u32[]{:S(2)}, u32[]{:S(2)}) collective-permute-start(bf16[4,8,4,16,512]{4,3,2,1,0:T(8,128)(2,1)S(1)} %all_to_all.31.own_ref), channel_id=1, source_target_pairs={{0,8},{8,0},{1,9},{9,1},{2,10},{10,2},{3,11},{11,3},{4,12},{12,4},... | collective-permute-start | bytes 6291464 | tf_op jit(solution)/shard_map/ppermute | solution.py:26
  70.5 41.7 %collective-permute-start.1 = (bf16[768,1024]{1,0:T(8,128)(2,1)}, bf16[768,1024]{1,0:T(8,128)(2,1)}, u32[]{:S(2)}, u32[]{:S(2)}) collective-permute-start(bf16[768,1024]{1,0:T(8,128)(2,1)} %docs_ref), channel_id=1, source_target_pairs={{0,64},{64,0},{1,65},{65,1},{2,66},{66,2},{3,67},{67,3},{4,68},{68... | collective-permute-start | bytes 4718600 | tf_op jit(solution)/shard_map/ppermute | solution.py:26
  77.3 44.9 %copy-start.1 = (bf16[4,512,128]{2,1,0:T(8,128)(2,1)}, bf16[4,512,128]{2,1,0:T(8,128)(2,1)S(1)}, u32[]{:S(2)}) copy-start(bf16[4,512,128]{2,1,0:T(8,128)(2,1)S(1)} %constant_dynamic-slice_fusion.second_ref) | copy-start | bytes 1572868
  122.3 1.0 copy-start.2
  123.3 0.8 copy-start.4
  134.0 6.1 %copy-start.5 = (s32[768]{0:T(1024)S(1)}, s32[768]{0:T(1024)}, u32[]{:S(2)}) copy-start(s32[768]{0:T(1024)} %param.7) | copy-start | bytes 9220
  134.1 21.6 %copy-start.6 = (s32[8]{0:T(128)S(1)}, s32[8]{0:T(128)}, u32[]{:S(2)}) copy-start(s32[8]{0:T(128)} %param.10) | copy-start | bytes 100
  135.1 12.5 %all-to-all-start.2 = ((bf16[8,240,128]{2,1,0:T(8,128)(2,1)}), bf16[8,240,128]{2,1,0:T(8,128)(2,1)S(1)}, u32[]{:S(2)}, u32[]{:S(2)}) async-start(bf16[8,240,128]{2,1,0:T(8,128)(2,1)} %pad_maximum_fusion), calls=%async_computation.2 | async-start | bytes 983040 | tf_op jit(solution)/shard_map/all_to_all | solution.py:18
  147.7 13.8 %collective-permute-start.2 = (bf16[288,128]{1,0:T(8,128)(2,1)S(1)}, bf16[288,128]{1,0:T(8,128)(2,1)S(1)}, u32[]{:S(2)}, u32[]{:S(2)}) collective-permute-start(bf16[288,128]{1,0:T(8,128)(2,1)S(1)} %pad_maximum_fusion.3), channel_id=1, source_target_pairs={{0,1},{1,0},{2,3},{3,2},{4,5},{5,4},{6,7},{7,6},{8,9},{9,8},{10,11... | collective-permute-start | bytes 221192 | tf_op jit(solution)/shard_map/ppermute | solution.py:26
  162.9 14.0 %all-to-all-start.4 = ((f32[8,2,8]{2,1,0:T(2,128)}), f32[8,2,8]{2,1,0:T(2,128)S(1)}, u32[]{:S(2)}, u32[]{:S(2)}) async-start(f32[8,2,8]{2,1,0:T(2,128)} %broadcast_in_dim.38), calls=%async_computation.4 | async-start | bytes 16384 | tf_op jit(solution)/shard_map/all_to_all | solution.py:18
  177.5 15.9 %all-to-all-start.5 = ((f32[8,2,8]{2,1,0:T(2,128)}), f32[8,2,8]{2,1,0:T(2,128)S(1)}, u32[]{:S(2)}, u32[]{:S(2)}) async-start(f32[8,2,8]{2,1,0:T(2,128)} %broadcast_in_dim.39), calls=%async_computation.5 | async-start | bytes 16384 | tf_op jit(solution)/shard_map/all_to_all | solution.py:18
  194.1 9.5 %all-to-all-start.3 = ((bf16[4,192,128]{2,1,0:T(8,128)(2,1)}), bf16[4,192,128]{2,1,0:T(8,128)(2,1)S(1)}, u32[]{:S(2)}, u32[]{:S(2)}) async-start(bf16[4,192,128]{2,1,0:T(8,128)(2,1)} %broadcast_in_dim.37), calls=%async_computation.3 | async-start | bytes 393216 | tf_op jit(solution)/shard_map/all_to_all | solution.py:18

commit v2 on v1

v2 whole, which is shorter than its diff:
```python
import jax
import jax.numpy as jnp
import ml_dtypes
import numpy as np
from jax import lax
from jax.experimental import pallas as pl
from jax.experimental.pallas import tpu as pltpu
from jax.sharding import Mesh, PartitionSpec as P


F32 = jnp.float32
BF16 = jnp.bfloat16
LANES = 128


def exchange(blocks, axes):
    return lax.all_to_all(blocks, axes, split_axis=0, concat_axis=0, tiled=True)


def to_all(block, axes):
    return exchange(jnp.broadcast_to(block, (lax.axis_size(axes), *block.shape)), axes)


def swap(array, axis):
    return lax.ppermute(array, axis, [(0, 1), (1, 0)])


def grade_parts(classes):
    levels = np.arange(classes, dtype=np.float32)
    rest = (np.float32(2.0) * levels / np.float32(classes - 1) - np.float32(1.0)) * np.sqrt(np.float32(3.0 / classes))
    parts = np.zeros((classes, LANES), np.float32)
    for k in range(3):
        part = rest.astype(ml_dtypes.bfloat16).astype(np.float32)
        parts[:, k] = part
        rest = rest - part
    return parts.astype(ml_dtypes.bfloat16)


def score_kernel(base_ref, own_docs_ref, near_docs_ref, first_ref, second_ref, grades_ref, mean_ref, scores_ref, first, both, total, marks):
    member = pl.program_id(0)
    n_x, n_zc = first_ref.shape[0], first_ref.shape[1]
    _, depth = own_docs_ref.shape
    width = first.shape[-1]
    for x in range(n_x):
        for z in range(n_zc // 2):
            for core in range(2):
                first[z, x, core] = first_ref[x, 2 * z + core, 0]
    second = second_ref[0]
    direction = jnp.sum(jnp.dot(second, grades_ref[...], preferred_element_type=F32), axis=1, keepdims=True)
    high = direction.astype(BF16).astype(F32)
    low = direction - high
    lane = lax.broadcasted_iota(jnp.int32, (width, LANES), 1)
    along = jnp.where(lane == 2 * member, high, jnp.where(lane == 2 * member + 1, low, 0.0))
    both[:, :LANES] = second
    both[:, LANES:] = along.astype(BF16)

    @pl.when(member == 0)
    def _():
        total[...] = jnp.zeros_like(total)
        row = lax.broadcasted_iota(jnp.int32, marks.shape, 0)
        col = lax.broadcasted_iota(jnp.int32, marks.shape, 1)
        marks[...] = jnp.where(col // 2 == row, 1.0, 0.0).astype(F32)

    for k, docs_ref in enumerate((own_docs_ref, near_docs_ref)):
        weight = first[...].reshape(depth, width)
        hidden = jnp.maximum(jnp.dot(docs_ref[...], weight, preferred_element_type=F32), 0.0).astype(BF16)
        total[k] += jnp.dot(hidden, both[...], preferred_element_type=F32)

    @pl.when(member == pl.num_programs(0) - 1)
    def _():
        for k in range(2):
            mean_ref[k] = total[k, :, :LANES]
            scores_ref[k] = lax.dot_general(
                marks[...], total[k, :, LANES:], (((1,), (1,)), ((), ())),
                precision=lax.Precision.HIGHEST, preferred_element_type=F32,
            )


def score(base, own_docs, near_docs, first, second, grades):
    n_x, n_zc, members, rows, width = first.shape
    n_docs, depth = own_docs.shape
    whole = lambda m, b: (0, 0)
    return pl.pallas_call(
        score_kernel,
        grid_spec=pltpu.PrefetchScalarGridSpec(
            num_scalar_prefetch=1,
            grid=(members,),
            in_specs=[
                pl.BlockSpec((n_docs, depth), whole),
                pl.BlockSpec((n_docs, depth), whole),
                pl.BlockSpec((n_x, n_zc, 1, rows, width), lambda m, b: (0, 0, m, 0, 0)),
                pl.BlockSpec((1, width, LANES), lambda m, b: (b[0] + m, 0, 0)),
                pl.BlockSpec((LANES, LANES), whole),
            ],
            out_specs=[
                pl.BlockSpec((2, n_docs, LANES), lambda m, b: (0, 0, 0)),
                pl.BlockSpec((2, 8, n_docs), lambda m, b: (0, 0, 0)),
            ],
            scratch_shapes=[
                pltpu.VMEM((n_zc // 2, n_x, 2, rows, width), BF16),
                pltpu.VMEM((width, 2 * LANES), BF16),
                pltpu.VMEM((2, n_docs, 2 * LANES), F32),
                pltpu.VMEM((8, LANES), F32),
            ],
        ),
        out_shape=[jax.ShapeDtypeStruct((2, n_docs, LANES), F32), jax.ShapeDtypeStruct((2, 8, n_docs), F32)],
        compiler_params=pltpu.CompilerParams(dimension_semantics=("arbitrary",), vmem_limit_bytes=40 * 1024 * 1024),
    )(base, own_docs, near_docs, first, second, grades)


def halves(scores):
    high = lax.reduce_precision(scores, 8, 7)
    low = lax.reduce_precision(scores - high, 8, 7)
    return jnp.stack([high, low]).astype(BF16)


def step(embeddings, valid_mask, first_weight, second_weight, thresholds):
    members, rows, width = first_weight.shape
    n_docs = embeddings.shape[0]
    z_axes = ("za", "zp")
    n_za, n_y = lax.axis_size("za"), lax.axis_size("y")
    parity, core = lax.axis_index("zp"), lax.axis_index("core")
    half, pair = members // 2, members // 4

    blocks = first_weight.reshape(1, 4, pair, rows, width)
    blocks = jnp.broadcast_to(blocks, (n_za, *blocks.shape[1:])).reshape(n_za * 4, pair, rows, width)
    along_z = exchange(blocks, ("za", "zp", "core"))
    docs, along_z = lax.optimization_barrier((embeddings, along_z))
    docs_near = swap(docs, "zp")
    first_a = to_all(along_z, "x")
    first_b = swap(first_a, "core")
    grades = jnp.asarray(grade_parts(second_weight.shape[2]))

    def scored(first, which):
        base = (parity * half + which * pair).reshape(1).astype(jnp.int32)
        return score(base, docs, docs_near, first, second_weight, grades)

    mean_a, scores_a = scored(first_a, core)
    mean_b, scores_b = scored(first_b, 1 - core)

    quarter = n_docs // n_y
    score_rows = half * n_docs // LANES
    scores_a, scores_b = scores_a[:, :pair], scores_b[:, :pair]
    low_core = core == 0
    scores = jnp.concatenate([jnp.where(low_core, scores_a, scores_b), jnp.where(low_core, scores_b, scores_a)], axis=1)
    parts = jnp.moveaxis(halves(scores), 0, 1).reshape(2, 1, 2 * score_rows, LANES)
    parts = jnp.broadcast_to(parts, (2, n_y, 2 * score_rows, LANES))
    packed = jnp.concatenate([(mean_a + mean_b).astype(BF16).reshape(2, n_y, quarter, LANES), parts], axis=2)
    even = parity == 0
    blocks = jnp.concatenate([jnp.where(even, packed[0], packed[1]), jnp.where(even, packed[1], packed[0])], axis=0)
    blocks = exchange(blocks, ("zp", "y"))
    part_mean = lax.reduce_precision(jnp.sum(blocks[:, :quarter].astype(F32), axis=0), 8, 7).astype(BF16)
    part_scores = blocks[:, quarter:].astype(F32).reshape(2, n_y * 2, score_rows, LANES).sum(axis=1)
    packed_scores = halves(part_scores.reshape(2 * score_rows, LANES)).reshape(4 * score_rows, LANES)
    message = jnp.concatenate([part_mean, packed_scores], axis=0)
    answer = swap(message, "zh")
    total = message.astype(F32) + answer.astype(F32)
    mean_quarter = (total[:quarter] * (1.0 / members)).astype(BF16)
    turn = [mean_quarter]
    for k in range(1, n_y):
        turn.append(lax.ppermute(mean_quarter, "y", [(i, (i + k) % n_y) for i in range(n_y)]))
    back = [(lax.axis_index("y") + n_y - q) % n_y for q in range(n_y)]
    mean_logits = jnp.concatenate([lax.select_n(k, *turn).astype(F32) for k in back], axis=0)
    scores = (total[quarter : quarter + 2 * score_rows] + total[quarter + 2 * score_rows :]).reshape(members, n_docs)

    cutoffs = thresholds.astype(F32) / 256.0
    validity = valid_mask.astype(F32)
    kept_soft = validity[None, :] * jax.nn.sigmoid(4.0 * (scores - cutoffs[:, None]))
    ens_score = jnp.sum(scores, axis=0) / members
    ens_kept = jax.nn.sigmoid(4.0 * (ens_score - jnp.mean(cutoffs)))
    counts = jnp.stack([jnp.sum(kept_soft, axis=1), jnp.sum(kept_soft * ens_kept[None, :], axis=1)])
    counts = to_all(counts, ("x", "core")).sum(axis=0)
    counts = to_all(counts, z_axes).sum(axis=0)
    member = lax.axis_index("y") * 2 + lax.axis_index("zh")
    shares = lax.dynamic_slice_in_dim(counts, member, 1, 1) / n_docs
    return mean_logits, shares[0], shares[1]


def solution(mesh):
    devices = mesh.devices.reshape(4, 2, 4, 2, 4, 2)
    fine = Mesh(devices, ("za", "zp", "x", "core", "y", "zh"))
    dp, ens = ("za", "zp", "x", "core"), ("y", "zh")
    return jax.shard_map(
        step,
        mesh=fine,
        in_specs=(P(dp, None), P(dp), P(None, dp, ens), P(None, ens, None), P()),
        out_specs=(P(dp, None), P(ens), P(ens)),
        check_vma=False,
    )
```

time: 206 us -> 194 us (0.942)
  blocking collectives: 58.5 us -> 70.6 us
  waiting for transfers between devices: 65.3 us -> 53.2 us
  starting transfers between devices: 50 us -> 42.7 us
  Pallas kernels: 19.8 us -> 16.4 us
    all_to_all x4 -> x3, waiting for transfers between devices: 25.9 us -> 11.7 us  [exchange(): return lax.all_to_all(blocks, axes, split_axis=0, concat_axis=0, tiled=True)]
    all_to_all x2, blocking collectives: 58.5 us -> 70.6 us  [exchange(): return lax.all_to_all(blocks, axes, split_axis=0, concat_axis=0, tiled=True)]
    ppermute x3, starting transfers between devices: 24.7 us -> 13.1 us  [swap(): return lax.ppermute(array, axis, [(0, 1), (1, 0)])]
    ppermute x0 -> x3, starting transfers between devices: none -> 10.2 us  [step(): lax.ppermute(mean_quarter, 'y', [(i, (i + k) % n_y) for i in range(n_y)])]
    all_to_all x4 -> x3, starting transfers between devices: 25.3 us -> 19.4 us  [exchange(): return lax.all_to_all(blocks, axes, split_axis=0, concat_axis=0, tiled=True)]
    pallas_call x2, Pallas kernels: 19.8 us -> 16.4 us  [score(): pl.pallas_call(score_kernel, grid_spec=pltpu.PrefetchScalarGridSpec(num_s...]
  transfers between devices with their start and end apart: 7 -> 9, of which waited for: 6 -> 5; matrix products, arithmetic and copies ran while one was open for 1% -> 1% of each run, Pallas kernels for 0% -> 4%
where the time goes in v2:
time: 194 us; the launch traced here: 192 us
  blocking collectives  70.6 us (36%)
  waiting for transfers between devices  53.2 us (27%)
  starting transfers between devices  42.7 us (22%)
  Pallas kernels  16.4 us (8%)
  local copies, waits for them, and re-layouts  4.26 us (2%)
  other arithmetic  3.2 us (2%)
    all_to_all x2, blocking collectives, exchange(): return lax.all_to_all(blocks, axes, split_axis=0, concat_axis=0, tiled=True)  70.6 us
    ppermute x3, waiting for transfers between devices, swap(): return lax.ppermute(array, axis, [(0, 1), (1, 0)])  40 us
    all_to_all x3, starting transfers between devices, exchange(): return lax.all_to_all(blocks, axes, split_axis=0, concat_axis=0, tiled=True)  19.4 us
    pallas_call x2, Pallas kernels, score(): pl.pallas_call(score_kernel, grid_spec=pltpu.PrefetchScalarGridSpec(num_s...  16.4 us
    ppermute x3, starting transfers between devices, swap(): return lax.ppermute(array, axis, [(0, 1), (1, 0)])  13.1 us
    all_to_all x3, waiting for transfers between devices, exchange(): return lax.all_to_all(blocks, axes, split_axis=0, concat_axis=0, tiled=True)  11.7 us
    ppermute x3, starting transfers between devices, step(): lax.ppermute(mean_quarter, 'y', [(i, (i + k) % n_y) for i in range(n_y)])  10.2 us
  transfers between devices with their start and end apart: 9, of which 5 were waited for; matrix products, arithmetic and copies ran while one was open for 1% of the time, Pallas kernels for 4%

profile of v2, /device:TPU:1, one launch (start us, length us, event | category | flops | bytes accessed | tf_op | source)
XLA Modules:
  0.0 192.1 jit_solution(676313366877764312)
XLA Ops:
  0.6 1.0 broadcast_in_dim.27
  1.6 40.1 %all_to_all.25 = bf16[16,2,16,512]{3,2,1,0:T(8,128)(2,1)S(1)} all-to-all(bf16[16,2,16,512]{3,2,1,0:T(8,128)(2,1)S(1)} %bitcast.30), channel_id=1, replica_groups=mesh['za'=4,'zp'=2,'x'=4,'core'=2,'y'=4,'zh'=2] {'za','zp','core'}, dimensions={0} | all-to-all | bytes 1048576 | tf_op jit(solution)/shard_map/all_to_all | solution.py:17
  41.6 0.3 broadcast_in_dim.28
  41.9 0.0 copy-start
  41.9 0.0 copy-start.3
  41.9 30.6 %all_to_all.26.first_ref = bf16[4,16,2,16,512]{4,3,2,1,0:T(8,128)(2,1)S(1)} all-to-all(bf16[4,16,2,16,512]{4,3,2,1,0:T(8,128)(2,1)S(1)} %broadcast_in_dim.28), channel_id=1, replica_groups=mesh['za'=4,'zp'=2,'x'=4,'core'=2,'y'=4,'zh'=2] {'x'}, dimensions={0} | all-to-all | bytes 4194304 | tf_op jit(solution)/shard_map/all_to_all | solution.py:17
  72.5 2.6 %collective-permute-start.1 = (bf16[4,16,2,16,512]{4,3,2,1,0:T(8,128)(2,1)S(1)}, bf16[4,16,2,16,512]{4,3,2,1,0:T(8,128)(2,1)}, u32[]{:S(2)}, u32[]{:S(2)}) collective-permute-start(bf16[4,16,2,16,512]{4,3,2,1,0:T(8,128)(2,1)S(1)} %all_to_all.26.first_ref), channel_id=1, source_target_pairs={{0,8},{8,0},{1,9},{9,1},{2,10},{10,2},{3,11},{11,3},{4,12},{12,4},... | collective-permute-start | bytes 6291464 | tf_op jit(solution)/shard_map/ppermute | solution.py:25
  75.1 2.5 %collective-permute-start = (bf16[768,1024]{1,0:T(8,128)(2,1)}, bf16[768,1024]{1,0:T(8,128)(2,1)}, u32[]{:S(2)}, u32[]{:S(2)}) collective-permute-start(bf16[768,1024]{1,0:T(8,128)(2,1)} %own_docs_ref.1), channel_id=1, source_target_pairs={{0,64},{64,0},{1,65},{65,1},{2,66},{66,2},{3,67},{67,3},{4,68},{68... | collective-permute-start | bytes 4718600 | tf_op jit(solution)/shard_map/ppermute | solution.py:25
  77.6 35.6 %collective-permute-done.near_docs_ref = bf16[768,1024]{1,0:T(8,128)(2,1)} collective-permute-done((bf16[768,1024]{1,0:T(8,128)(2,1)}, bf16[768,1024]{1,0:T(8,128)(2,1)}, u32[]{:S(2)}, u32[]{:S(2)}) %collective-permute-start) | collective-permute-done | bytes 1572896 | tf_op jit(solution)/shard_map/ppermute | solution.py:25
  113.2 0.0 copy-done
  113.2 0.0 copy-done.3
  113.2 8.1 %shard_map.85 = (f32[2,768,128]{2,1,0:T(8,128)S(1)}, f32[2,8,768]{2,1,0:T(8,128)S(1)}) custom-call(s32[1]{0:T(128)} %bitcast.base_ref, bf16[768,1024]{1,0:T(8,128)(2,1)} %own_docs_ref.1, bf16[768,1024]{1,0:T(8,128)(2,1)} %collective-permute-done.near_docs_ref, bf16[4,16,2,16,512]{4,3,2,1,0:T(8,128)(2,1)S(1)} %all_to_all.26.first_ref, ...), custom_call_target="tpu_custom_call" | custom-call | tf_op jit(solution)/shard_map/pallas_call | solution.py:83
  121.3 0.0 copy-start.1
  121.3 0.9 copy-done.1
  122.2 0.0 collective-permute-done.1.first_ref
  122.2 0.0 copy-start.2
  122.2 8.4 %shard_map.86 = (f32[2,768,128]{2,1,0:T(8,128)S(1)}, f32[2,8,768]{2,1,0:T(8,128)S(1)}) custom-call(s32[1]{0:T(128)} %bitcast.3.base_ref, bf16[768,1024]{1,0:T(8,128)(2,1)} %own_docs_ref.1, bf16[768,1024]{1,0:T(8,128)(2,1)} %collective-permute-done.near_docs_ref, bf16[4,16,2,16,512]{4,3,2,1,0:T(8,128)(2,1)} %collective-permute-done.1.first_ref, ...), custom_call_target="tpu_custom_call" | custom-call | tf_op jit(solution)/shard_map/pallas_call | solution.py:83
  130.7 0.0 copy-done.2
  130.7 0.0 copy-start.4
  130.7 0.1 add_convert_fusion
  130.8 0.0 copy-start.5
  130.9 0.1 select_bitcast_fusion.1
  131.0 0.8 pad_maximum_fusion
  131.8 4.2 %all-to-all-start.2 = ((bf16[8,240,128]{2,1,0:T(8,128)(2,1)}), bf16[8,240,128]{2,1,0:T(8,128)(2,1)S(1)}, u32[]{:S(2)}, u32[]{:S(2)}) async-start(bf16[8,240,128]{2,1,0:T(8,128)(2,1)} %pad_maximum_fusion), calls=%async_computation.2 | async-start | bytes 983040 | tf_op jit(solution)/shard_map/all_to_all | solution.py:17
  136.0 0.0 copy-done.4
  136.0 7.1 %all-to-all-done.2 = bf16[8,240,128]{2,1,0:T(8,128)(2,1)S(1)} async-done(((bf16[8,240,128]{2,1,0:T(8,128)(2,1)}), bf16[8,240,128]{2,1,0:T(8,128)(2,1)S(1)}, u32[]{:S(2)}, u32[]{:S(2)}) %all-to-all-start.2) | async-done | bytes 491552 | tf_op jit(solution)/shard_map/all_to_all | solution.py:17
  143.1 0.1 convert_reduce_fusion
  143.2 8.0 %collective-permute-start.2 = (bf16[288,128]{1,0:T(8,128)(2,1)S(1)}, bf16[288,128]{1,0:T(8,128)(2,1)S(1)}, u32[]{:S(2)}, u32[]{:S(2)}) collective-permute-start(bf16[288,128]{1,0:T(8,128)(2,1)S(1)} %pad_maximum_fusion.2), channel_id=1, source_target_pairs={{0,1},{1,0},{2,3},{3,2},{4,5},{5,4},{6,7},{7,6},{8,9},{9,8},{10,11... | collective-permute-start | bytes 221192 | tf_op jit(solution)/shard_map/ppermute | solution.py:25
  151.2 0.0 copy-done.5
  151.2 0.6 fusion.6
  151.8 0.1 sub.63
  151.9 0.1 sub.64
  152.7 4.4 %collective-permute-done.2 = bf16[288,128]{1,0:T(8,128)(2,1)S(1)} collective-permute-done((bf16[288,128]{1,0:T(8,128)(2,1)S(1)}, bf16[288,128]{1,0:T(8,128)(2,1)S(1)}, u32[]{:S(2)}, u32[]{:S(2)}) %collective-permute-start.2) | collective-permute-done | bytes 73760 | tf_op jit(solution)/shard_map/ppermute | solution.py:25
  157.1 0.1 divide_multiply_fusion
  157.3 0.1 fusion.7
  157.4 0.1 reduce_sum.89
  157.5 0.1 reduce_sum.90
  157.6 0.1 reduce_sum.94
  157.7 0.1 reduce_sum.95
  157.8 0.6 broadcast_in_dim.31
  158.4 9.3 %all-to-all-start.3 = ((f32[8,2,8]{2,1,0:T(2,128)}), f32[8,2,8]{2,1,0:T(2,128)S(1)}, u32[]{:S(2)}, u32[]{:S(2)}) async-start(f32[8,2,8]{2,1,0:T(2,128)} %broadcast_in_dim.31), calls=%async_computation.3 | async-start | bytes 16384 | tf_op jit(solution)/shard_map/all_to_all | solution.py:17
  167.7 4.6 %all-to-all-done.3 = f32[8,2,8]{2,1,0:T(2,128)S(1)} async-done(((f32[8,2,8]{2,1,0:T(2,128)}), f32[8,2,8]{2,1,0:T(2,128)S(1)}, u32[]{:S(2)}, u32[]{:S(2)}) %all-to-all-start.3) | async-done | bytes 544 | tf_op jit(solution)/shard_map/all_to_all | solution.py:17
  172.3 0.6 broadcast_in_dim.32
  172.9 5.9 %all-to-all-start.4 = ((f32[8,2,8]{2,1,0:T(2,128)}), f32[8,2,8]{2,1,0:T(2,128)S(1)}, u32[]{:S(2)}, u32[]{:S(2)}) async-start(f32[8,2,8]{2,1,0:T(2,128)} %broadcast_in_dim.32), calls=%async_computation.4 | async-start | bytes 16384 | tf_op jit(solution)/shard_map/all_to_all | solution.py:17
  178.9 3.8 %collective-permute-start.3 = (bf16[192,128]{1,0:T(8,128)(2,1)S(1)}, bf16[192,128]{1,0:T(8,128)(2,1)S(1)}, u32[]{:S(2)}, u32[]{:S(2)}) collective-permute-start(bf16[192,128]{1,0:T(8,128)(2,1)S(1)} %fusion.1), channel_id=1, source_target_pairs={{0,2},{2,4},{4,6},{6,0},{1,3},{3,5},{5,7},{7,1},{8,10},{10,12},{12... | collective-permute-start | bytes 147464 | tf_op jit(solution)/shard_map/ppermute | solution.py:161
  182.7 3.7 %collective-permute-start.4 = (bf16[192,128]{1,0:T(8,128)(2,1)S(1)}, bf16[192,128]{1,0:T(8,128)(2,1)S(1)}, u32[]{:S(2)}, u32[]{:S(2)}) collective-permute-start(bf16[192,128]{1,0:T(8,128)(2,1)S(1)} %fusion.1), channel_id=1, source_target_pairs={{0,4},{2,6},{4,0},{6,2},{1,5},{3,7},{5,1},{7,3},{8,12},{10,14},{12... | collective-permute-start | bytes 147464 | tf_op jit(solution)/shard_map/ppermute | solution.py:161
  186.4 2.7 %collective-permute-start.5 = (bf16[192,128]{1,0:T(8,128)(2,1)S(1)}, bf16[192,128]{1,0:T(8,128)(2,1)S(1)}, u32[]{:S(2)}, u32[]{:S(2)}) collective-permute-start(bf16[192,128]{1,0:T(8,128)(2,1)S(1)} %fusion.1), channel_id=1, source_target_pairs={{0,6},{2,0},{4,2},{6,4},{1,7},{3,1},{5,3},{7,5},{8,14},{10,8},{12,... | collective-permute-start | bytes 147464 | tf_op jit(solution)/shard_map/ppermute | solution.py:161
  189.1 0.0 all-to-all-done.4
  189.2 0.1 dynamic-slice_multiply_fusion
  189.2 0.5 fusion.8
  189.8 0.0 collective-permute-done.3
  189.8 0.0 collective-permute-done.4
  189.8 1.5 collective-permute-done.5
  191.3 0.8 maximum_convert_fusion
  (26 shorter events, 0.3 us)
Async XLA Ops:
  41.9 71.3 %copy-start = (bf16[8,512,128]{2,1,0:T(8,128)(2,1)S(1)}, bf16[8,512,128]{2,1,0:T(8,128)(2,1)}, u32[]{:S(2)}) copy-start(bf16[8,512,128]{2,1,0:T(8,128)(2,1)} %second_ref.3) | copy-start | bytes 3145732
  41.9 71.3 %copy-start.3 = (bf16[128,128]{1,0:T(8,128)(2,1)S(1)}, bf16[128,128]{1,0:T(8,128)(2,1)}, u32[]{:S(2)}) copy-start(bf16[128,128]{1,0:T(8,128)(2,1)} %constant.76.clone.grades_ref) | copy-start | bytes 98308
  72.5 49.7 %collective-permute-start.1 = (bf16[4,16,2,16,512]{4,3,2,1,0:T(8,128)(2,1)S(1)}, bf16[4,16,2,16,512]{4,3,2,1,0:T(8,128)(2,1)}, u32[]{:S(2)}, u32[]{:S(2)}) collective-permute-start(bf16[4,16,2,16,512]{4,3,2,1,0:T(8,128)(2,1)S(1)} %all_to_all.26.first_ref), channel_id=1, source_target_pairs={{0,8},{8,0},{1,9},{9,1},{2,10},{10,2},{3,11},{11,3},{4,12},{12,4},... | collective-permute-start | bytes 6291464 | tf_op jit(solution)/shard_map/ppermute | solution.py:25
  75.1 38.1 %collective-permute-start = (bf16[768,1024]{1,0:T(8,128)(2,1)}, bf16[768,1024]{1,0:T(8,128)(2,1)}, u32[]{:S(2)}, u32[]{:S(2)}) collective-permute-start(bf16[768,1024]{1,0:T(8,128)(2,1)} %own_docs_ref.1), channel_id=1, source_target_pairs={{0,64},{64,0},{1,65},{65,1},{2,66},{66,2},{3,67},{67,3},{4,68},{68... | collective-permute-start | bytes 4718600 | tf_op jit(solution)/shard_map/ppermute | solution.py:25
  121.3 0.9 copy-start.1
  122.2 8.5 %copy-start.2 = (f32[2,768,128]{2,1,0:T(8,128)S(1)}, f32[2,768,128]{2,1,0:T(8,128)}, u32[]{:S(2)}) copy-start(f32[2,768,128]{2,1,0:T(8,128)} %copy-done.1) | copy-start | bytes 2359300
  130.7 5.3 %copy-start.4 = (s32[768]{0:T(1024)S(1)}, s32[768]{0:T(1024)}, u32[]{:S(2)}) copy-start(s32[768]{0:T(1024)} %param.7) | copy-start | bytes 9220
  130.8 20.4 %copy-start.5 = (s32[8]{0:T(128)S(1)}, s32[8]{0:T(128)}, u32[]{:S(2)}) copy-start(s32[8]{0:T(128)} %param.10) | copy-start | bytes 100
  131.8 11.3 %all-to-all-start.2 = ((bf16[8,240,128]{2,1,0:T(8,128)(2,1)}), bf16[8,240,128]{2,1,0:T(8,128)(2,1)S(1)}, u32[]{:S(2)}, u32[]{:S(2)}) async-start(bf16[8,240,128]{2,1,0:T(8,128)(2,1)} %pad_maximum_fusion), calls=%async_computation.2 | async-start | bytes 983040 | tf_op jit(solution)/shard_map/all_to_all | solution.py:17
  143.2 13.8 %collective-permute-start.2 = (bf16[288,128]{1,0:T(8,128)(2,1)S(1)}, bf16[288,128]{1,0:T(8,128)(2,1)S(1)}, u32[]{:S(2)}, u32[]{:S(2)}) collective-permute-start(bf16[288,128]{1,0:T(8,128)(2,1)S(1)} %pad_maximum_fusion.2), channel_id=1, source_target_pairs={{0,1},{1,0},{2,3},{3,2},{4,5},{5,4},{6,7},{7,6},{8,9},{9,8},{10,11... | collective-permute-start | bytes 221192 | tf_op jit(solution)/shard_map/ppermute | solution.py:25
  158.4 13.9 %all-to-all-start.3 = ((f32[8,2,8]{2,1,0:T(2,128)}), f32[8,2,8]{2,1,0:T(2,128)S(1)}, u32[]{:S(2)}, u32[]{:S(2)}) async-start(f32[8,2,8]{2,1,0:T(2,128)} %broadcast_in_dim.31), calls=%async_computation.3 | async-start | bytes 16384 | tf_op jit(solution)/shard_map/all_to_all | solution.py:17
  172.9 16.2 %all-to-all-start.4 = ((f32[8,2,8]{2,1,0:T(2,128)}), f32[8,2,8]{2,1,0:T(2,128)S(1)}, u32[]{:S(2)}, u32[]{:S(2)}) async-start(f32[8,2,8]{2,1,0:T(2,128)} %broadcast_in_dim.32), calls=%async_computation.4 | async-start | bytes 16384 | tf_op jit(solution)/shard_map/all_to_all | solution.py:17
  178.9 10.9 %collective-permute-start.3 = (bf16[192,128]{1,0:T(8,128)(2,1)S(1)}, bf16[192,128]{1,0:T(8,128)(2,1)S(1)}, u32[]{:S(2)}, u32[]{:S(2)}) collective-permute-start(bf16[192,128]{1,0:T(8,128)(2,1)S(1)} %fusion.1), channel_id=1, source_target_pairs={{0,2},{2,4},{4,6},{6,0},{1,3},{3,5},{5,7},{7,1},{8,10},{10,12},{12... | collective-permute-start | bytes 147464 | tf_op jit(solution)/shard_map/ppermute | solution.py:161
  182.7 7.0 %collective-permute-start.4 = (bf16[192,128]{1,0:T(8,128)(2,1)S(1)}, bf16[192,128]{1,0:T(8,128)(2,1)S(1)}, u32[]{:S(2)}, u32[]{:S(2)}) collective-permute-start(bf16[192,128]{1,0:T(8,128)(2,1)S(1)} %fusion.1), channel_id=1, source_target_pairs={{0,4},{2,6},{4,0},{6,2},{1,5},{3,7},{5,1},{7,3},{8,12},{10,14},{12... | collective-permute-start | bytes 147464 | tf_op jit(solution)/shard_map/ppermute | solution.py:161
  186.4 4.8 %collective-permute-start.5 = (bf16[192,128]{1,0:T(8,128)(2,1)S(1)}, bf16[192,128]{1,0:T(8,128)(2,1)S(1)}, u32[]{:S(2)}, u32[]{:S(2)}) collective-permute-start(bf16[192,128]{1,0:T(8,128)(2,1)S(1)} %fusion.1), channel_id=1, source_target_pairs={{0,6},{2,0},{4,2},{6,4},{1,7},{3,1},{5,3},{7,5},{8,14},{10,8},{12,... | collective-permute-start | bytes 147464 | tf_op jit(solution)/shard_map/ppermute | solution.py:161

commit v3 on v2

v3 whole, which is shorter than its diff:
```python
import functools

import jax
import jax.numpy as jnp
import ml_dtypes
import numpy as np
from jax import lax
from jax.experimental import pallas as pl
from jax.experimental.pallas import tpu as pltpu
from jax.sharding import Mesh, PartitionSpec as P


F32 = jnp.float32
BF16 = jnp.bfloat16


def exchange(blocks, axes):
    return lax.all_to_all(blocks, axes, split_axis=0, concat_axis=0, tiled=True)


def to_all(block, axes):
    return exchange(jnp.broadcast_to(block, (lax.axis_size(axes), *block.shape)), axes)


def swap(array, axis):
    return lax.ppermute(array, axis, [(0, 1), (1, 0)])


def grade_rows(classes):
    levels = np.arange(classes, dtype=np.float32)
    rest = (np.float32(2.0) * levels / np.float32(classes - 1) - np.float32(1.0)) * np.sqrt(np.float32(3.0 / classes))
    rows = np.zeros((classes + 8, classes), np.float32)
    rows[:classes] = np.eye(classes)
    for k in range(3):
        rows[classes + k] = rest.astype(ml_dtypes.bfloat16).astype(np.float32)
        rest = rest - rows[classes + k]
    return rows.astype(ml_dtypes.bfloat16)


CROSS = (((1,), (1,)), ((), ()))


def score_kernel(last, scalars, own_docs_ref, near_docs_hbm, first_ref, second_ref, grades_ref, *refs):
    if last:
        before_ref, packed_ref, total, first, both, near_docs, arrived = refs
        own_docs = own_docs_ref
    else:
        total, first, both, near_docs, arrived, own_docs, own_arrived = refs
        fetch_own = pltpu.make_async_copy(own_docs_ref, own_docs, own_arrived)
    member = pl.program_id(0)
    which, parity = scalars[1], scalars[2]
    n_x, n_zc = first_ref.shape[0], first_ref.shape[1]
    _, depth = near_docs.shape
    width = first.shape[-1]
    classes = second_ref.shape[-1]
    fetch_near = pltpu.make_async_copy(near_docs_hbm, near_docs, arrived)

    @pl.when(member == 0)
    def _():
        if not last:
            fetch_own.start()
        fetch_near.start()

    at = 0 if last else member
    for x in range(n_x):
        for z in range(n_zc // 2):
            for core in range(2):
                first[z, x, core] = first_ref[x, 2 * z + core, at]
    rows = lax.dot_general(grades_ref[...], second_ref[0], CROSS, preferred_element_type=F32)
    direction = rows[classes : classes + 1] + rows[classes + 1 : classes + 2] + rows[classes + 2 : classes + 3]
    high = direction.astype(BF16).astype(F32)
    low = direction - high
    row = lax.broadcasted_iota(jnp.int32, (8, width), 0)
    slot = 2 * which + member
    along = jnp.where(row == slot, high, jnp.where(row == slot + 4, low, 0.0))
    both[...] = jnp.concatenate([rows[:classes], along], axis=0).astype(BF16)

    def add(k, docs):
        weight = first[...].reshape(depth, width)
        hidden = jnp.maximum(jnp.dot(docs, weight, preferred_element_type=F32), 0.0).astype(BF16)
        part = lax.dot_general(both[...], hidden, CROSS, preferred_element_type=F32)

        @pl.when(member == 0)
        def _():
            total[k] = part + before_ref[k] if last else part

        @pl.when(member > 0)
        def _():
            total[k] += part

    if not last:

        @pl.when(member == 0)
        def _():
            fetch_own.wait()

    add(0, own_docs[...])

    @pl.when(member == 0)
    def _():
        fetch_near.wait()

    add(1, near_docs[...])
    if not last:
        return

    @pl.when(member == pl.num_programs(0) - 1)
    def _():
        n_y = packed_ref.shape[0] // 2
        quarter = classes // n_y
        for k in range(2):
            owner = (parity if k == 0 else 1 - parity) * n_y
            scores = total[k, classes : classes + 4] + total[k, classes + 4 : classes + 8]
            top = scores.astype(BF16).astype(F32)
            parts = jnp.concatenate([top, scores - top], axis=0).astype(BF16)
            for q in range(n_y):
                packed_ref[owner + q, :quarter] = total[k, quarter * q : quarter * (q + 1)].astype(BF16)
                packed_ref[owner + q, quarter:] = parts


def score(last, scalars, own_docs, near_docs, first, second, grades, n_y, *before):
    n_x, n_zc, members, rows, width = first.shape
    n_docs, depth = own_docs.shape
    classes = second.shape[-1]
    vmem = pl.BlockSpec(memory_space=pltpu.VMEM)
    hbm = pl.BlockSpec(memory_space=pltpu.HBM)
    totals = (2, classes + 8, n_docs)
    packed = (2 * n_y, classes // n_y + 8, n_docs)
    first_spec = pl.BlockSpec((n_x, n_zc, 1, rows, width), lambda m, s: (0, 0, m, 0, 0)) if last else vmem
    docs_scratch = [pltpu.VMEM((n_docs, depth), BF16), pltpu.SemaphoreType.DMA]
    scratch = [pltpu.VMEM((n_zc // 2, n_x, 2, rows, width), BF16), pltpu.VMEM((classes + 8, width), BF16)] + docs_scratch
    return pl.pallas_call(
        functools.partial(score_kernel, last),
        grid_spec=pltpu.PrefetchScalarGridSpec(
            num_scalar_prefetch=1,
            grid=(members,),
            in_specs=[
                vmem if last else hbm,
                hbm,
                first_spec,
                pl.BlockSpec((1, width, classes), lambda m, s: (s[0] + m, 0, 0)),
                vmem,
            ]
            + [vmem] * len(before),
            out_specs=vmem,
            scratch_shapes=[pltpu.VMEM(totals, F32)] + scratch if last else scratch + docs_scratch,
        ),
        out_shape=jax.ShapeDtypeStruct(packed, BF16) if last else jax.ShapeDtypeStruct(totals, F32),
        compiler_params=pltpu.CompilerParams(dimension_semantics=("arbitrary",), vmem_limit_bytes=32 * 1024 * 1024),
    )(scalars, own_docs, near_docs, first, second, grades, *before)


def order_kernel(mine, *refs):
    *turn, out_ref = refs
    n_y = len(turn)
    quarters = []
    for q in range(n_y):
        back = lax.rem(mine[0] + n_y - q, n_y)
        quarter = turn[0][...].astype(F32)
        for k in range(1, n_y):
            quarter = jnp.where(back == k, turn[k][...].astype(F32), quarter)
        quarters.append(quarter)
    out_ref[...] = jnp.concatenate(quarters, axis=0).T


def in_order(mine, turn):
    rows, n_docs = turn[0].shape
    vmem = pl.BlockSpec(memory_space=pltpu.VMEM)
    return pl.pallas_call(
        order_kernel,
        in_specs=[pl.BlockSpec(memory_space=pltpu.SMEM)] + [vmem] * len(turn),
        out_specs=vmem,
        out_shape=jax.ShapeDtypeStruct((n_docs, rows * len(turn)), F32),
        compiler_params=pltpu.CompilerParams(vmem_limit_bytes=8 * 1024 * 1024),
    )(mine.reshape(1).astype(jnp.int32), *turn)


def halves(scores):
    high = lax.reduce_precision(scores, 8, 7)
    low = lax.reduce_precision(scores - high, 8, 7)
    return jnp.stack([high, low]).astype(BF16)


def step(embeddings, valid_mask, first_weight, second_weight, thresholds):
    members, rows, width = first_weight.shape
    n_docs = embeddings.shape[0]
    z_axes = ("za", "zp")
    n_za, n_y = lax.axis_size("za"), lax.axis_size("y")
    parity, core = lax.axis_index("zp"), lax.axis_index("core")
    half, pair = members // 2, members // 4

    blocks = first_weight.reshape(1, 4, pair, rows, width)
    blocks = jnp.broadcast_to(blocks, (n_za, *blocks.shape[1:])).reshape(n_za * 4, pair, rows, width)
    along_z = exchange(blocks, ("za", "zp", "core"))
    docs, along_z = lax.optimization_barrier((embeddings, along_z))
    docs_near = swap(docs, "zp")
    first_a = to_all(along_z, "x")
    first_b = swap(first_a, "core")
    classes = second_weight.shape[2]
    grades = jnp.asarray(grade_rows(classes))

    def scored(last, first, which, *before):
        scalars = jnp.stack([parity * half + which * pair, which, parity]).astype(jnp.int32)
        return score(last, scalars, docs, docs_near, first, second_weight, grades, n_y, *before)

    total_a = scored(False, first_a, core)
    packed = scored(True, first_b, 1 - core, total_a)

    quarter = classes // n_y
    blocks = exchange(packed, ("zp", "y"))
    part_mean = lax.reduce_precision(jnp.sum(blocks[:, :quarter].astype(F32), axis=0), 8, 7).astype(BF16)
    part_scores = blocks[:, quarter:].astype(F32).reshape(2, n_y, 2, half, n_docs).sum(axis=(1, 2)).reshape(members, n_docs)
    message = jnp.concatenate([part_mean, halves(part_scores).reshape(2 * members, n_docs)], axis=0)
    answer = swap(message, "zh")
    total = message.astype(F32) + answer.astype(F32)
    mean_quarter = (total[:quarter] * (1.0 / members)).astype(BF16)
    turn = [mean_quarter]
    for k in range(1, n_y):
        turn.append(lax.ppermute(mean_quarter, "y", [(i, (i + k) % n_y) for i in range(n_y)]))
    mean_logits = in_order(lax.axis_index("y"), turn)
    scores = total[quarter : quarter + members] + total[quarter + members :]

    cutoffs = thresholds.astype(F32) / 256.0
    validity = valid_mask.astype(F32)
    kept_soft = validity[None, :] * jax.nn.sigmoid(4.0 * (scores - cutoffs[:, None]))
    ens_score = jnp.sum(scores, axis=0) / members
    ens_kept = jax.nn.sigmoid(4.0 * (ens_score - jnp.mean(cutoffs)))
    counts = jnp.stack([jnp.sum(kept_soft, axis=1), jnp.sum(kept_soft * ens_kept[None, :], axis=1)])
    counts = to_all(counts, ("x", "core")).sum(axis=0)
    counts = to_all(counts, z_axes).sum(axis=0)
    member = lax.axis_index("y") * 2 + lax.axis_index("zh")
    shares = lax.dynamic_slice_in_dim(counts, member, 1, 1) / n_docs
    return mean_logits, shares[0], shares[1]


def solution(mesh):
    devices = mesh.devices.reshape(4, 2, 4, 2, 4, 2)
    fine = Mesh(devices, ("za", "zp", "x", "core", "y", "zh"))
    dp, ens = ("za", "zp", "x", "core"), ("y", "zh")
    return jax.shard_map(
        step,
        mesh=fine,
        in_specs=(P(dp, None), P(dp), P(None, dp, ens), P(None, ens, None), P()),
        out_specs=(P(dp, None), P(ens), P(ens)),
        check_vma=False,
    )
```

time: 194 us -> 191 us (0.985)
  blocking collectives: 70.6 us -> 82.3 us
  waiting for transfers between devices: 53.2 us -> 46 us
  starting transfers between devices: 42.7 us -> 37.8 us
    all_to_all x2 -> x3, blocking collectives: 70.6 us -> 82.3 us  [exchange(): return lax.all_to_all(blocks, axes, split_axis=0, concat_axis=0, tiled=True)]
    all_to_all x3 -> x2, waiting for transfers between devices: 11.7 us -> 4.87 us  [exchange(): return lax.all_to_all(blocks, axes, split_axis=0, concat_axis=0, tiled=True)]
    all_to_all x3 -> x2, starting transfers between devices: 19.4 us -> 15.7 us  [exchange(): return lax.all_to_all(blocks, axes, split_axis=0, concat_axis=0, tiled=True)]
    pallas_call x2 -> x3, Pallas kernels: 16.4 us -> 16.9 us  [the longest x2 16 us: score(): pl.pallas_call(functools.partial(score_kernel, last), grid_spec=pltpu.Pre...]
  transfers between devices with their start and end apart: 9 -> 8, of which waited for: 5 -> 5; matrix products, arithmetic and copies ran while one was open for 1% -> 1% of each run, Pallas kernels for 4% -> 4%
where the time goes in v3:
time: 191 us; the launch traced here: 189 us
  blocking collectives  82.3 us (43%)
  waiting for transfers between devices  46 us (24%)
  starting transfers between devices  37.8 us (20%)
  Pallas kernels  16.9 us (9%)
  local copies, waits for them, and re-layouts  3.04 us (2%)
    all_to_all x3, blocking collectives, exchange(): return lax.all_to_all(blocks, axes, split_axis=0, concat_axis=0, tiled=True)  82.3 us
    ppermute x3, waiting for transfers between devices, swap(): return lax.ppermute(array, axis, [(0, 1), (1, 0)])  40.1 us
    pallas_call x2, Pallas kernels, score(): pl.pallas_call(functools.partial(score_kernel, last), grid_spec=pltpu.Pre...  16 us
    all_to_all x2, starting transfers between devices, exchange(): return lax.all_to_all(blocks, axes, split_axis=0, concat_axis=0, tiled=True)  15.7 us
    ppermute x3, starting transfers between devices, swap(): return lax.ppermute(array, axis, [(0, 1), (1, 0)])  13.1 us
    ppermute x3, starting transfers between devices, step(): lax.ppermute(mean_quarter, 'y', [(i, (i + k) % n_y) for i in range(n_y)])  9.03 us
    all_to_all x2, waiting for transfers between devices, exchange(): return lax.all_to_all(blocks, axes, split_axis=0, concat_axis=0, tiled=True)  4.87 us
  transfers between devices with their start and end apart: 8, of which 5 were waited for; matrix products, arithmetic and copies ran while one was open for 1% of the time, Pallas kernels for 4%

profile of v3, /device:TPU:1, one launch (start us, length us, event | category | flops | bytes accessed | tf_op | source)
XLA Modules:
  0.0 188.9 jit_solution(8335681034961481857)
XLA Ops:
  0.6 1.0 broadcast_in_dim.20
  1.6 40.1 %all_to_all.25 = bf16[16,2,16,512]{3,2,1,0:T(8,128)(2,1)S(1)} all-to-all(bf16[16,2,16,512]{3,2,1,0:T(8,128)(2,1)S(1)} %bitcast.14), channel_id=1, replica_groups=mesh['za'=4,'zp'=2,'x'=4,'core'=2,'y'=4,'zh'=2] {'za','zp','core'}, dimensions={0} | all-to-all | bytes 1048576 | tf_op jit(solution)/shard_map/all_to_all | solution.py:18
  41.6 0.3 broadcast_in_dim.21
  41.9 0.0 copy-start
  41.9 0.0 copy-start.1
  41.9 30.6 %all_to_all.26.first_ref = bf16[4,16,2,16,512]{4,3,2,1,0:T(8,128)(2,1)S(1)} all-to-all(bf16[4,16,2,16,512]{4,3,2,1,0:T(8,128)(2,1)S(1)} %broadcast_in_dim.21), channel_id=1, replica_groups=mesh['za'=4,'zp'=2,'x'=4,'core'=2,'y'=4,'zh'=2] {'x'}, dimensions={0} | all-to-all | bytes 4194304 | tf_op jit(solution)/shard_map/all_to_all | solution.py:18
  72.5 2.6 %collective-permute-start.1 = (bf16[4,16,2,16,512]{4,3,2,1,0:T(8,128)(2,1)S(1)}, bf16[4,16,2,16,512]{4,3,2,1,0:T(8,128)(2,1)}, u32[]{:S(2)}, u32[]{:S(2)}) collective-permute-start(bf16[4,16,2,16,512]{4,3,2,1,0:T(8,128)(2,1)S(1)} %all_to_all.26.first_ref), channel_id=1, source_target_pairs={{0,8},{8,0},{1,9},{9,1},{2,10},{10,2},{3,11},{11,3},{4,12},{12,4},... | collective-permute-start | bytes 6291464 | tf_op jit(solution)/shard_map/ppermute | solution.py:26
  75.1 2.5 %collective-permute-start = (bf16[768,1024]{1,0:T(8,128)(2,1)}, bf16[768,1024]{1,0:T(8,128)(2,1)}, u32[]{:S(2)}, u32[]{:S(2)}) collective-permute-start(bf16[768,1024]{1,0:T(8,128)(2,1)} %own_docs_ref.1), channel_id=1, source_target_pairs={{0,64},{64,0},{1,65},{65,1},{2,66},{66,2},{3,67},{67,3},{4,68},{68... | collective-permute-start | bytes 4718600 | tf_op jit(solution)/shard_map/ppermute | solution.py:26
  77.6 0.1 add_add_fusion.scalars
  77.7 0.1 add_add_fusion.1.scalars
  77.8 35.4 %collective-permute-done.near_docs_hbm = bf16[768,1024]{1,0:T(8,128)(2,1)} collective-permute-done((bf16[768,1024]{1,0:T(8,128)(2,1)}, bf16[768,1024]{1,0:T(8,128)(2,1)}, u32[]{:S(2)}, u32[]{:S(2)}) %collective-permute-start) | collective-permute-done | bytes 1572896 | tf_op jit(solution)/shard_map/ppermute | solution.py:26
  113.2 0.0 copy-done
  113.2 0.0 copy-done.1
  113.2 7.7 %shard_map.85.refs_0_ = f32[2,136,768]{2,1,0:T(8,128)S(1)} custom-call(s32[3]{0:T(128)S(1)} %add_add_fusion.1.scalars, bf16[768,1024]{1,0:T(8,128)(2,1)} %own_docs_ref.1, bf16[768,1024]{1,0:T(8,128)(2,1)} %collective-permute-done.near_docs_hbm, bf16[4,16,2,16,512]{4,3,2,1,0:T(8,128)(2,1)S(1)} %all_to_all.26.first_ref, bf16[8,512,128]{2,1,0:T(8,128)(2,1)S(1)} %copy-done, ...), custom_call_target="tpu_custom_call" | custom-call | tf_op jit(solution)/shard_map/pallas_call | solution.py:132
  121.0 0.0 collective-permute-done.1.first_ref
  121.0 8.3 %shard_map.86 = bf16[8,40,768]{2,1,0:T(8,128)(2,1)S(1)} custom-call(s32[3]{0:T(128)S(1)} %add_add_fusion.scalars, bf16[768,1024]{1,0:T(8,128)(2,1)} %own_docs_ref.1, bf16[768,1024]{1,0:T(8,128)(2,1)} %collective-permute-done.near_docs_hbm, bf16[4,16,2,16,512]{4,3,2,1,0:T(8,128)(2,1)} %collective-permute-done.1.first_ref, bf16[8,512,128]{2,1,0:T(8,128)(2,1)S(1)} %copy-done, ...), custom_call_target="tpu_custom_call" | custom-call | tf_op jit(solution)/shard_map/pallas_call | solution.py:132
  129.2 0.0 copy-start.3
  129.2 0.0 copy-start.2
  129.3 11.7 %all_to_all.27 = bf16[8,40,768]{2,1,0:T(8,128)(2,1)S(1)} all-to-all(bf16[8,40,768]{2,1,0:T(8,128)(2,1)S(1)} %shard_map.86), channel_id=1, replica_groups=mesh['za'=4,'zp'=2,'x'=4,'core'=2,'y'=4,'zh'=2] {'zp','y'}, dimensions={0} | all-to-all | bytes 983040 | tf_op jit(solution)/shard_map/all_to_all | solution.py:18
  141.0 0.1 reshape.69
  141.1 0.1 convert_reduce_fusion
  141.2 7.9 %collective-permute-start.2 = (bf16[48,768]{1,0:T(8,128)(2,1)S(1)}, bf16[48,768]{1,0:T(8,128)(2,1)S(1)}, u32[]{:S(2)}, u32[]{:S(2)}) collective-permute-start(bf16[48,768]{1,0:T(8,128)(2,1)S(1)} %pad_maximum_fusion), channel_id=1, source_target_pairs={{0,1},{1,0},{2,3},{3,2},{4,5},{5,4},{6,7},{7,6},{8,9},{9,8},{10,11... | collective-permute-start | bytes 221192 | tf_op jit(solution)/shard_map/ppermute | solution.py:26
  149.2 0.0 copy-done.3
  149.2 0.6 fusion.4
  149.8 0.0 copy-done.2
  150.4 4.6 %collective-permute-done.2 = bf16[48,768]{1,0:T(8,128)(2,1)S(1)} collective-permute-done((bf16[48,768]{1,0:T(8,128)(2,1)S(1)}, bf16[48,768]{1,0:T(8,128)(2,1)S(1)}, u32[]{:S(2)}, u32[]{:S(2)}) %collective-permute-start.2) | collective-permute-done | bytes 73760 | tf_op jit(solution)/shard_map/ppermute | solution.py:26
  155.1 0.1 fusion.3
  155.2 0.2 fusion.5
  155.4 0.6 broadcast_in_dim.22
  156.0 7.3 %all-to-all-start.3 = ((f32[8,2,8]{2,1,0:T(2,128)}), f32[8,2,8]{2,1,0:T(2,128)S(1)}, u32[]{:S(2)}, u32[]{:S(2)}) async-start(f32[8,2,8]{2,1,0:T(2,128)} %broadcast_in_dim.22), calls=%async_computation.3 | async-start | bytes 16384 | tf_op jit(solution)/shard_map/all_to_all | solution.py:18
  163.3 4.6 %all-to-all-done.3 = f32[8,2,8]{2,1,0:T(2,128)S(1)} async-done(((f32[8,2,8]{2,1,0:T(2,128)}), f32[8,2,8]{2,1,0:T(2,128)S(1)}, u32[]{:S(2)}, u32[]{:S(2)}) %all-to-all-start.3) | async-done | bytes 544 | tf_op jit(solution)/shard_map/all_to_all | solution.py:18
  168.0 0.6 broadcast_in_dim.23
  168.6 8.4 %all-to-all-start.4 = ((f32[8,2,8]{2,1,0:T(2,128)}), f32[8,2,8]{2,1,0:T(2,128)S(1)}, u32[]{:S(2)}, u32[]{:S(2)}) async-start(f32[8,2,8]{2,1,0:T(2,128)} %broadcast_in_dim.23), calls=%async_computation.4 | async-start | bytes 16384 | tf_op jit(solution)/shard_map/all_to_all | solution.py:18
  177.0 1.9 %collective-permute-start.3 = (bf16[32,768]{1,0:T(8,128)(2,1)S(1)}, bf16[32,768]{1,0:T(8,128)(2,1)S(1)}, u32[]{:S(2)}, u32[]{:S(2)}) collective-permute-start(bf16[32,768]{1,0:T(8,128)(2,1)S(1)} %fusion.refs_0_), channel_id=1, source_target_pairs={{0,2},{2,4},{4,6},{6,0},{1,3},{3,5},{5,7},{7,1},{8,10},{10,12},{12... | collective-permute-start | bytes 147464 | tf_op jit(solution)/shard_map/ppermute | solution.py:219
  178.9 4.1 %collective-permute-start.4 = (bf16[32,768]{1,0:T(8,128)(2,1)S(1)}, bf16[32,768]{1,0:T(8,128)(2,1)S(1)}, u32[]{:S(2)}, u32[]{:S(2)}) collective-permute-start(bf16[32,768]{1,0:T(8,128)(2,1)S(1)} %fusion.refs_0_), channel_id=1, source_target_pairs={{0,4},{2,6},{4,0},{6,2},{1,5},{3,7},{5,1},{7,3},{8,12},{10,14},{12... | collective-permute-start | bytes 147464 | tf_op jit(solution)/shard_map/ppermute | solution.py:219
  183.0 3.0 %collective-permute-start.5 = (bf16[32,768]{1,0:T(8,128)(2,1)S(1)}, bf16[32,768]{1,0:T(8,128)(2,1)S(1)}, u32[]{:S(2)}, u32[]{:S(2)}) collective-permute-start(bf16[32,768]{1,0:T(8,128)(2,1)S(1)} %fusion.refs_0_), channel_id=1, source_target_pairs={{0,6},{2,0},{4,2},{6,4},{1,7},{3,1},{5,3},{7,5},{8,14},{10,8},{12,... | collective-permute-start | bytes 147464 | tf_op jit(solution)/shard_map/ppermute | solution.py:219
  186.0 0.2 all-to-all-done.4
  186.3 0.1 dynamic-slice_multiply_fusion
  186.4 0.5 fusion.6
  186.9 0.0 collective-permute-done.3.refs_1_
  186.9 0.0 collective-permute-done.4.refs_2_
  186.9 1.1 collective-permute-done.5.refs_3_
  188.0 0.9 shard_map.87
  (14 shorter events, 0.2 us)
Async XLA Ops:
  41.9 71.3 %copy-start = (bf16[8,512,128]{2,1,0:T(8,128)(2,1)S(1)}, bf16[8,512,128]{2,1,0:T(8,128)(2,1)}, u32[]{:S(2)}) copy-start(bf16[8,512,128]{2,1,0:T(8,128)(2,1)} %second_ref.3) | copy-start | bytes 3145732
  41.9 71.3 %copy-start.1 = (bf16[136,128]{1,0:T(8,128)(2,1)S(1)}, bf16[136,128]{1,0:T(8,128)(2,1)}, u32[]{:S(2)}) copy-start(bf16[136,128]{1,0:T(8,128)(2,1)} %constant.47.clone.grades_ref) | copy-start | bytes 104452
  72.5 48.5 %collective-permute-start.1 = (bf16[4,16,2,16,512]{4,3,2,1,0:T(8,128)(2,1)S(1)}, bf16[4,16,2,16,512]{4,3,2,1,0:T(8,128)(2,1)}, u32[]{:S(2)}, u32[]{:S(2)}) collective-permute-start(bf16[4,16,2,16,512]{4,3,2,1,0:T(8,128)(2,1)S(1)} %all_to_all.26.first_ref), channel_id=1, source_target_pairs={{0,8},{8,0},{1,9},{9,1},{2,10},{10,2},{3,11},{11,3},{4,12},{12,4},... | collective-permute-start | bytes 6291464 | tf_op jit(solution)/shard_map/ppermute | solution.py:26
  75.1 38.1 %collective-permute-start = (bf16[768,1024]{1,0:T(8,128)(2,1)}, bf16[768,1024]{1,0:T(8,128)(2,1)}, u32[]{:S(2)}, u32[]{:S(2)}) collective-permute-start(bf16[768,1024]{1,0:T(8,128)(2,1)} %own_docs_ref.1), channel_id=1, source_target_pairs={{0,64},{64,0},{1,65},{65,1},{2,66},{66,2},{3,67},{67,3},{4,68},{68... | collective-permute-start | bytes 4718600 | tf_op jit(solution)/shard_map/ppermute | solution.py:26
  129.2 19.9 %copy-start.3 = (s32[8]{0:T(128)S(1)}, s32[8]{0:T(128)}, u32[]{:S(2)}) copy-start(s32[8]{0:T(128)} %param.10) | copy-start | bytes 100
  129.2 20.5 %copy-start.2 = (s32[768]{0:T(1024)S(1)}, s32[768]{0:T(1024)}, u32[]{:S(2)}) copy-start(s32[768]{0:T(1024)} %param.7) | copy-start | bytes 9220
  141.2 13.8 %collective-permute-start.2 = (bf16[48,768]{1,0:T(8,128)(2,1)S(1)}, bf16[48,768]{1,0:T(8,128)(2,1)S(1)}, u32[]{:S(2)}, u32[]{:S(2)}) collective-permute-start(bf16[48,768]{1,0:T(8,128)(2,1)S(1)} %pad_maximum_fusion), channel_id=1, source_target_pairs={{0,1},{1,0},{2,3},{3,2},{4,5},{5,4},{6,7},{7,6},{8,9},{9,8},{10,11... | collective-permute-start | bytes 221192 | tf_op jit(solution)/shard_map/ppermute | solution.py:26
  156.0 12.0 %all-to-all-start.3 = ((f32[8,2,8]{2,1,0:T(2,128)}), f32[8,2,8]{2,1,0:T(2,128)S(1)}, u32[]{:S(2)}, u32[]{:S(2)}) async-start(f32[8,2,8]{2,1,0:T(2,128)} %broadcast_in_dim.22), calls=%async_computation.3 | async-start | bytes 16384 | tf_op jit(solution)/shard_map/all_to_all | solution.py:18
  168.6 17.7 %all-to-all-start.4 = ((f32[8,2,8]{2,1,0:T(2,128)}), f32[8,2,8]{2,1,0:T(2,128)S(1)}, u32[]{:S(2)}, u32[]{:S(2)}) async-start(f32[8,2,8]{2,1,0:T(2,128)} %broadcast_in_dim.23), calls=%async_computation.4 | async-start | bytes 16384 | tf_op jit(solution)/shard_map/all_to_all | solution.py:18
  177.0 9.9 %collective-permute-start.3 = (bf16[32,768]{1,0:T(8,128)(2,1)S(1)}, bf16[32,768]{1,0:T(8,128)(2,1)S(1)}, u32[]{:S(2)}, u32[]{:S(2)}) collective-permute-start(bf16[32,768]{1,0:T(8,128)(2,1)S(1)} %fusion.refs_0_), channel_id=1, source_target_pairs={{0,2},{2,4},{4,6},{6,0},{1,3},{3,5},{5,7},{7,1},{8,10},{10,12},{12... | collective-permute-start | bytes 147464 | tf_op jit(solution)/shard_map/ppermute | solution.py:219
  178.9 8.0 %collective-permute-start.4 = (bf16[32,768]{1,0:T(8,128)(2,1)S(1)}, bf16[32,768]{1,0:T(8,128)(2,1)S(1)}, u32[]{:S(2)}, u32[]{:S(2)}) collective-permute-start(bf16[32,768]{1,0:T(8,128)(2,1)S(1)} %fusion.refs_0_), channel_id=1, source_target_pairs={{0,4},{2,6},{4,0},{6,2},{1,5},{3,7},{5,1},{7,3},{8,12},{10,14},{12... | collective-permute-start | bytes 147464 | tf_op jit(solution)/shard_map/ppermute | solution.py:219
  183.0 5.0 %collective-permute-start.5 = (bf16[32,768]{1,0:T(8,128)(2,1)S(1)}, bf16[32,768]{1,0:T(8,128)(2,1)S(1)}, u32[]{:S(2)}, u32[]{:S(2)}) collective-permute-start(bf16[32,768]{1,0:T(8,128)(2,1)S(1)} %fusion.refs_0_), channel_id=1, source_target_pairs={{0,6},{2,0},{4,2},{6,4},{1,7},{3,1},{5,3},{7,5},{8,14},{10,8},{12,... | collective-permute-start | bytes 147464 | tf_op jit(solution)/shard_map/ppermute | solution.py:219

commit v4 on v3

--- a/solution.py
+++ b/solution.py
@@ -45,8 +45,8 @@
         before_ref, packed_ref, total, first, both, near_docs, arrived = refs
         own_docs = own_docs_ref
     else:
-        total, first, both, near_docs, arrived, own_docs, own_arrived = refs
-        fetch_own = pltpu.make_async_copy(own_docs_ref, own_docs, own_arrived)
+        total, first, both, near_docs, arrived = refs
+        own_docs = own_docs_ref
     member = pl.program_id(0)
     which, parity = scalars[1], scalars[2]
     n_x, n_zc = first_ref.shape[0], first_ref.shape[1]
@@ -57,8 +57,6 @@
 
     @pl.when(member == 0)
     def _():
-        if not last:
-            fetch_own.start()
         fetch_near.start()
 
     at = 0 if last else member
@@ -87,12 +85,6 @@
         @pl.when(member > 0)
         def _():
             total[k] += part
-
-    if not last:
-
-        @pl.when(member == 0)
-        def _():
-            fetch_own.wait()
 
     add(0, own_docs[...])
 
@@ -135,7 +127,7 @@
             num_scalar_prefetch=1,
             grid=(members,),
             in_specs=[
-                vmem if last else hbm,
+                vmem,
                 hbm,
                 first_spec,
                 pl.BlockSpec((1, width, classes), lambda m, s: (s[0] + m, 0, 0)),
@@ -143,10 +135,10 @@
             ]
             + [vmem] * len(before),
             out_specs=vmem,
-            scratch_shapes=[pltpu.VMEM(totals, F32)] + scratch if last else scratch + docs_scratch,
+            scratch_shapes=[pltpu.VMEM(totals, F32)] * last + scratch,
         ),
         out_shape=jax.ShapeDtypeStruct(packed, BF16) if last else jax.ShapeDtypeStruct(totals, F32),
-        compiler_params=pltpu.CompilerParams(dimension_semantics=("arbitrary",), vmem_limit_bytes=32 * 1024 * 1024),
+        compiler_params=pltpu.CompilerParams(dimension_semantics=("arbitrary",), vmem_limit_bytes=14 * 1024 * 1024),
     )(scalars, own_docs, near_docs, first, second, grades, *before)
 
 
@@ -192,7 +184,7 @@
     blocks = first_weight.reshape(1, 4, pair, rows, width)
     blocks = jnp.broadcast_to(blocks, (n_za, *blocks.shape[1:])).reshape(n_za * 4, pair, rows, width)
     along_z = exchange(blocks, ("za", "zp", "core"))
-    docs, along_z = lax.optimization_barrier((embeddings, along_z))
+    docs = embeddings
     docs_near = swap(docs, "zp")
     first_a = to_all(along_z, "x")
     first_b = swap(first_a, "core")

time: 191 us -> 191 us (level)
  no operation moved by 1% of the time
where the time goes in v4:
time: 191 us; the launch traced here: 189 us
  blocking collectives  82.3 us (43%)
  waiting for transfers between devices  46 us (24%)
  starting transfers between devices  37.9 us (20%)
  Pallas kernels  17 us (9%)
  local copies, waits for them, and re-layouts  3.04 us (2%)
    all_to_all x3, blocking collectives, exchange(): return lax.all_to_all(blocks, axes, split_axis=0, concat_axis=0, tiled=True)  82.3 us
    ppermute x3, waiting for transfers between devices, swap(): return lax.ppermute(array, axis, [(0, 1), (1, 0)])  40.1 us
    pallas_call x2, Pallas kernels, score(): pl.pallas_call(functools.partial(score_kernel, last), grid_spec=pltpu.Pre...  16.1 us
    all_to_all x2, starting transfers between devices, exchange(): return lax.all_to_all(blocks, axes, split_axis=0, concat_axis=0, tiled=True)  15.8 us
    ppermute x3, starting transfers between devices, swap(): return lax.ppermute(array, axis, [(0, 1), (1, 0)])  13.1 us
    ppermute x3, starting transfers between devices, step(): lax.ppermute(mean_quarter, 'y', [(i, (i + k) % n_y) for i in range(n_y)])  9.02 us
    all_to_all x2, waiting for transfers between devices, exchange(): return lax.all_to_all(blocks, axes, split_axis=0, concat_axis=0, tiled=True)  4.87 us
  transfers between devices with their start and end apart: 8, of which 5 were waited for; matrix products, arithmetic and copies ran while one was open for 1% of the time, Pallas kernels for 4%

profile of v4, /device:TPU:1, one launch (start us, length us, event | category | flops | bytes accessed | tf_op | source)
XLA Modules:
  0.0 189.0 jit_solution(7850104686676840894)
XLA Ops:
  0.6 1.0 broadcast_in_dim.20
  1.6 40.1 %all_to_all.25 = bf16[16,2,16,512]{3,2,1,0:T(8,128)(2,1)S(1)} all-to-all(bf16[16,2,16,512]{3,2,1,0:T(8,128)(2,1)S(1)} %bitcast.14), channel_id=1, replica_groups=mesh['za'=4,'zp'=2,'x'=4,'core'=2,'y'=4,'zh'=2] {'za','zp','core'}, dimensions={0} | all-to-all | bytes 1048576 | tf_op jit(solution)/shard_map/all_to_all | solution.py:18
  41.6 0.3 broadcast_in_dim.21
  41.9 0.0 copy-start
  41.9 0.0 copy-start.1
  41.9 30.6 %all_to_all.26.first_ref = bf16[4,16,2,16,512]{4,3,2,1,0:T(8,128)(2,1)S(1)} all-to-all(bf16[4,16,2,16,512]{4,3,2,1,0:T(8,128)(2,1)S(1)} %broadcast_in_dim.21), channel_id=1, replica_groups=mesh['za'=4,'zp'=2,'x'=4,'core'=2,'y'=4,'zh'=2] {'x'}, dimensions={0} | all-to-all | bytes 4194304 | tf_op jit(solution)/shard_map/all_to_all | solution.py:18
  72.5 2.6 %collective-permute-start.1 = (bf16[4,16,2,16,512]{4,3,2,1,0:T(8,128)(2,1)S(1)}, bf16[4,16,2,16,512]{4,3,2,1,0:T(8,128)(2,1)}, u32[]{:S(2)}, u32[]{:S(2)}) collective-permute-start(bf16[4,16,2,16,512]{4,3,2,1,0:T(8,128)(2,1)S(1)} %all_to_all.26.first_ref), channel_id=1, source_target_pairs={{0,8},{8,0},{1,9},{9,1},{2,10},{10,2},{3,11},{11,3},{4,12},{12,4},... | collective-permute-start | bytes 6291464 | tf_op jit(solution)/shard_map/ppermute | solution.py:26
  75.1 2.5 %collective-permute-start = (bf16[768,1024]{1,0:T(8,128)(2,1)}, bf16[768,1024]{1,0:T(8,128)(2,1)}, u32[]{:S(2)}, u32[]{:S(2)}) collective-permute-start(bf16[768,1024]{1,0:T(8,128)(2,1)} %own_docs_ref.3), channel_id=1, source_target_pairs={{0,64},{64,0},{1,65},{65,1},{2,66},{66,2},{3,67},{67,3},{4,68},{68... | collective-permute-start | bytes 4718600 | tf_op jit(solution)/shard_map/ppermute | solution.py:26
  77.6 0.1 add_add_fusion.scalars
  77.7 0.1 add_add_fusion.1.scalars
  77.8 35.4 %collective-permute-done.near_docs_hbm = bf16[768,1024]{1,0:T(8,128)(2,1)} collective-permute-done((bf16[768,1024]{1,0:T(8,128)(2,1)}, bf16[768,1024]{1,0:T(8,128)(2,1)}, u32[]{:S(2)}, u32[]{:S(2)}) %collective-permute-start) | collective-permute-done | bytes 1572896 | tf_op jit(solution)/shard_map/ppermute | solution.py:26
  113.2 0.0 copy-done
  113.2 0.0 copy-done.1
  113.2 7.8 %shard_map.85.refs_0_ = f32[2,136,768]{2,1,0:T(8,128)S(1)} custom-call(s32[3]{0:T(128)S(1)} %add_add_fusion.1.scalars, bf16[768,1024]{1,0:T(8,128)(2,1)} %own_docs_ref.3, bf16[768,1024]{1,0:T(8,128)(2,1)} %collective-permute-done.near_docs_hbm, bf16[4,16,2,16,512]{4,3,2,1,0:T(8,128)(2,1)S(1)} %all_to_all.26.first_ref, bf16[8,512,128]{2,1,0:T(8,128)(2,1)S(1)} %copy-done, ...), custom_call_target="tpu_custom_call" | custom-call | tf_op jit(solution)/shard_map/pallas_call | solution.py:124
  121.1 0.0 collective-permute-done.1.first_ref
  121.1 8.3 %shard_map.86 = bf16[8,40,768]{2,1,0:T(8,128)(2,1)S(1)} custom-call(s32[3]{0:T(128)S(1)} %add_add_fusion.scalars, bf16[768,1024]{1,0:T(8,128)(2,1)} %own_docs_ref.3, bf16[768,1024]{1,0:T(8,128)(2,1)} %collective-permute-done.near_docs_hbm, bf16[4,16,2,16,512]{4,3,2,1,0:T(8,128)(2,1)} %collective-permute-done.1.first_ref, bf16[8,512,128]{2,1,0:T(8,128)(2,1)S(1)} %copy-done, ...), custom_call_target="tpu_custom_call" | custom-call | tf_op jit(solution)/shard_map/pallas_call | solution.py:124
  129.3 0.0 copy-start.3
  129.4 0.0 copy-start.2
  129.4 11.7 %all_to_all.27 = bf16[8,40,768]{2,1,0:T(8,128)(2,1)S(1)} all-to-all(bf16[8,40,768]{2,1,0:T(8,128)(2,1)S(1)} %shard_map.86), channel_id=1, replica_groups=mesh['za'=4,'zp'=2,'x'=4,'core'=2,'y'=4,'zh'=2] {'zp','y'}, dimensions={0} | all-to-all | bytes 983040 | tf_op jit(solution)/shard_map/all_to_all | solution.py:18
  141.1 0.1 reshape.69
  141.2 0.1 convert_reduce_fusion
  141.3 7.9 %collective-permute-start.2 = (bf16[48,768]{1,0:T(8,128)(2,1)S(1)}, bf16[48,768]{1,0:T(8,128)(2,1)S(1)}, u32[]{:S(2)}, u32[]{:S(2)}) collective-permute-start(bf16[48,768]{1,0:T(8,128)(2,1)S(1)} %pad_maximum_fusion), channel_id=1, source_target_pairs={{0,1},{1,0},{2,3},{3,2},{4,5},{5,4},{6,7},{7,6},{8,9},{9,8},{10,11... | collective-permute-start | bytes 221192 | tf_op jit(solution)/shard_map/ppermute | solution.py:26
  149.2 0.0 copy-done.3
  149.3 0.6 fusion.4
  149.9 0.0 copy-done.2
  150.5 4.6 %collective-permute-done.2 = bf16[48,768]{1,0:T(8,128)(2,1)S(1)} collective-permute-done((bf16[48,768]{1,0:T(8,128)(2,1)S(1)}, bf16[48,768]{1,0:T(8,128)(2,1)S(1)}, u32[]{:S(2)}, u32[]{:S(2)}) %collective-permute-start.2) | collective-permute-done | bytes 73760 | tf_op jit(solution)/shard_map/ppermute | solution.py:26
  155.2 0.1 fusion.3
  155.3 0.2 fusion.5
  155.4 0.6 broadcast_in_dim.22
  156.0 7.3 %all-to-all-start.3 = ((f32[8,2,8]{2,1,0:T(2,128)}), f32[8,2,8]{2,1,0:T(2,128)S(1)}, u32[]{:S(2)}, u32[]{:S(2)}) async-start(f32[8,2,8]{2,1,0:T(2,128)} %broadcast_in_dim.22), calls=%async_computation.3 | async-start | bytes 16384 | tf_op jit(solution)/shard_map/all_to_all | solution.py:18
  163.4 4.6 %all-to-all-done.3 = f32[8,2,8]{2,1,0:T(2,128)S(1)} async-done(((f32[8,2,8]{2,1,0:T(2,128)}), f32[8,2,8]{2,1,0:T(2,128)S(1)}, u32[]{:S(2)}, u32[]{:S(2)}) %all-to-all-start.3) | async-done | bytes 544 | tf_op jit(solution)/shard_map/all_to_all | solution.py:18
  168.0 0.6 broadcast_in_dim.23
  168.6 8.4 %all-to-all-start.4 = ((f32[8,2,8]{2,1,0:T(2,128)}), f32[8,2,8]{2,1,0:T(2,128)S(1)}, u32[]{:S(2)}, u32[]{:S(2)}) async-start(f32[8,2,8]{2,1,0:T(2,128)} %broadcast_in_dim.23), calls=%async_computation.4 | async-start | bytes 16384 | tf_op jit(solution)/shard_map/all_to_all | solution.py:18
  177.1 1.9 %collective-permute-start.3 = (bf16[32,768]{1,0:T(8,128)(2,1)S(1)}, bf16[32,768]{1,0:T(8,128)(2,1)S(1)}, u32[]{:S(2)}, u32[]{:S(2)}) collective-permute-start(bf16[32,768]{1,0:T(8,128)(2,1)S(1)} %fusion.refs_0_), channel_id=1, source_target_pairs={{0,2},{2,4},{4,6},{6,0},{1,3},{3,5},{5,7},{7,1},{8,10},{10,12},{12... | collective-permute-start | bytes 147464 | tf_op jit(solution)/shard_map/ppermute | solution.py:211
  179.0 4.1 %collective-permute-start.4 = (bf16[32,768]{1,0:T(8,128)(2,1)S(1)}, bf16[32,768]{1,0:T(8,128)(2,1)S(1)}, u32[]{:S(2)}, u32[]{:S(2)}) collective-permute-start(bf16[32,768]{1,0:T(8,128)(2,1)S(1)} %fusion.refs_0_), channel_id=1, source_target_pairs={{0,4},{2,6},{4,0},{6,2},{1,5},{3,7},{5,1},{7,3},{8,12},{10,14},{12... | collective-permute-start | bytes 147464 | tf_op jit(solution)/shard_map/ppermute | solution.py:211
  183.1 3.0 %collective-permute-start.5 = (bf16[32,768]{1,0:T(8,128)(2,1)S(1)}, bf16[32,768]{1,0:T(8,128)(2,1)S(1)}, u32[]{:S(2)}, u32[]{:S(2)}) collective-permute-start(bf16[32,768]{1,0:T(8,128)(2,1)S(1)} %fusion.refs_0_), channel_id=1, source_target_pairs={{0,6},{2,0},{4,2},{6,4},{1,7},{3,1},{5,3},{7,5},{8,14},{10,8},{12,... | collective-permute-start | bytes 147464 | tf_op jit(solution)/shard_map/ppermute | solution.py:211
  186.1 0.2 all-to-all-done.4
  186.4 0.1 dynamic-slice_multiply_fusion
  186.5 0.5 fusion.6
  187.0 0.0 collective-permute-done.3.refs_1_
  187.0 0.0 collective-permute-done.4.refs_2_
  187.0 1.1 collective-permute-done.5.refs_3_
  188.1 0.9 shard_map.87
  (14 shorter events, 0.2 us)
Async XLA Ops:
  41.9 71.3 %copy-start = (bf16[8,512,128]{2,1,0:T(8,128)(2,1)S(1)}, bf16[8,512,128]{2,1,0:T(8,128)(2,1)}, u32[]{:S(2)}) copy-start(bf16[8,512,128]{2,1,0:T(8,128)(2,1)} %second_ref.3) | copy-start | bytes 3145732
  41.9 71.3 %copy-start.1 = (bf16[136,128]{1,0:T(8,128)(2,1)S(1)}, bf16[136,128]{1,0:T(8,128)(2,1)}, u32[]{:S(2)}) copy-start(bf16[136,128]{1,0:T(8,128)(2,1)} %constant.47.clone.grades_ref) | copy-start | bytes 104452
  72.5 48.6 %collective-permute-start.1 = (bf16[4,16,2,16,512]{4,3,2,1,0:T(8,128)(2,1)S(1)}, bf16[4,16,2,16,512]{4,3,2,1,0:T(8,128)(2,1)}, u32[]{:S(2)}, u32[]{:S(2)}) collective-permute-start(bf16[4,16,2,16,512]{4,3,2,1,0:T(8,128)(2,1)S(1)} %all_to_all.26.first_ref), channel_id=1, source_target_pairs={{0,8},{8,0},{1,9},{9,1},{2,10},{10,2},{3,11},{11,3},{4,12},{12,4},... | collective-permute-start | bytes 6291464 | tf_op jit(solution)/shard_map/ppermute | solution.py:26
  75.1 38.1 %collective-permute-start = (bf16[768,1024]{1,0:T(8,128)(2,1)}, bf16[768,1024]{1,0:T(8,128)(2,1)}, u32[]{:S(2)}, u32[]{:S(2)}) collective-permute-start(bf16[768,1024]{1,0:T(8,128)(2,1)} %own_docs_ref.3), channel_id=1, source_target_pairs={{0,64},{64,0},{1,65},{65,1},{2,66},{66,2},{3,67},{67,3},{4,68},{68... | collective-permute-start | bytes 4718600 | tf_op jit(solution)/shard_map/ppermute | solution.py:26
  129.3 19.9 %copy-start.3 = (s32[8]{0:T(128)S(1)}, s32[8]{0:T(128)}, u32[]{:S(2)}) copy-start(s32[8]{0:T(128)} %param.10) | copy-start | bytes 100
  129.4 20.5 %copy-start.2 = (s32[768]{0:T(1024)S(1)}, s32[768]{0:T(1024)}, u32[]{:S(2)}) copy-start(s32[768]{0:T(1024)} %param.7) | copy-start | bytes 9220
  141.3 13.8 %collective-permute-start.2 = (bf16[48,768]{1,0:T(8,128)(2,1)S(1)}, bf16[48,768]{1,0:T(8,128)(2,1)S(1)}, u32[]{:S(2)}, u32[]{:S(2)}) collective-permute-start(bf16[48,768]{1,0:T(8,128)(2,1)S(1)} %pad_maximum_fusion), channel_id=1, source_target_pairs={{0,1},{1,0},{2,3},{3,2},{4,5},{5,4},{6,7},{7,6},{8,9},{9,8},{10,11... | collective-permute-start | bytes 221192 | tf_op jit(solution)/shard_map/ppermute | solution.py:26
  156.0 12.0 %all-to-all-start.3 = ((f32[8,2,8]{2,1,0:T(2,128)}), f32[8,2,8]{2,1,0:T(2,128)S(1)}, u32[]{:S(2)}, u32[]{:S(2)}) async-start(f32[8,2,8]{2,1,0:T(2,128)} %broadcast_in_dim.22), calls=%async_computation.3 | async-start | bytes 16384 | tf_op jit(solution)/shard_map/all_to_all | solution.py:18
  168.6 17.7 %all-to-all-start.4 = ((f32[8,2,8]{2,1,0:T(2,128)}), f32[8,2,8]{2,1,0:T(2,128)S(1)}, u32[]{:S(2)}, u32[]{:S(2)}) async-start(f32[8,2,8]{2,1,0:T(2,128)} %broadcast_in_dim.23), calls=%async_computation.4 | async-start | bytes 16384 | tf_op jit(solution)/shard_map/all_to_all | solution.py:18
  177.1 9.9 %collective-permute-start.3 = (bf16[32,768]{1,0:T(8,128)(2,1)S(1)}, bf16[32,768]{1,0:T(8,128)(2,1)S(1)}, u32[]{:S(2)}, u32[]{:S(2)}) collective-permute-start(bf16[32,768]{1,0:T(8,128)(2,1)S(1)} %fusion.refs_0_), channel_id=1, source_target_pairs={{0,2},{2,4},{4,6},{6,0},{1,3},{3,5},{5,7},{7,1},{8,10},{10,12},{12... | collective-permute-start | bytes 147464 | tf_op jit(solution)/shard_map/ppermute | solution.py:211
  179.0 8.0 %collective-permute-start.4 = (bf16[32,768]{1,0:T(8,128)(2,1)S(1)}, bf16[32,768]{1,0:T(8,128)(2,1)S(1)}, u32[]{:S(2)}, u32[]{:S(2)}) collective-permute-start(bf16[32,768]{1,0:T(8,128)(2,1)S(1)} %fusion.refs_0_), channel_id=1, source_target_pairs={{0,4},{2,6},{4,0},{6,2},{1,5},{3,7},{5,1},{7,3},{8,12},{10,14},{12... | collective-permute-start | bytes 147464 | tf_op jit(solution)/shard_map/ppermute | solution.py:211
  183.1 5.0 %collective-permute-start.5 = (bf16[32,768]{1,0:T(8,128)(2,1)S(1)}, bf16[32,768]{1,0:T(8,128)(2,1)S(1)}, u32[]{:S(2)}, u32[]{:S(2)}) collective-permute-start(bf16[32,768]{1,0:T(8,128)(2,1)S(1)} %fusion.refs_0_), channel_id=1, source_target_pairs={{0,6},{2,0},{4,2},{6,4},{1,7},{3,1},{5,3},{7,5},{8,14},{10,8},{12,... | collective-permute-start | bytes 147464 | tf_op jit(solution)/shard_map/ppermute | solution.py:211

commit v5 on v4

--- a/solution.py
+++ b/solution.py
@@ -142,29 +142,46 @@
     )(scalars, own_docs, near_docs, first, second, grades, *before)
 
 
-def order_kernel(mine, *refs):
-    *turn, out_ref = refs
-    n_y = len(turn)
-    quarters = []
-    for q in range(n_y):
-        back = lax.rem(mine[0] + n_y - q, n_y)
-        quarter = turn[0][...].astype(F32)
-        for k in range(1, n_y):
-            quarter = jnp.where(back == k, turn[k][...].astype(F32), quarter)
-        quarters.append(quarter)
-    out_ref[...] = jnp.concatenate(quarters, axis=0).T
-
-
-def in_order(mine, turn):
-    rows, n_docs = turn[0].shape
+def stage_kernel(docs_hbm, out_ref, arrived):
+    fetch = pltpu.make_async_copy(docs_hbm, out_ref, arrived)
+    fetch.start()
+    fetch.wait()
+
+
+def staged(docs):
+    return pl.pallas_call(
+        stage_kernel,
+        in_specs=[pl.BlockSpec(memory_space=pltpu.HBM)],
+        out_specs=pl.BlockSpec(memory_space=pltpu.VMEM),
+        scratch_shapes=[pltpu.SemaphoreType.DMA],
+        out_shape=jax.ShapeDtypeStruct(docs.shape, docs.dtype),
+        compiler_params=pltpu.CompilerParams(vmem_limit_bytes=4 * 1024 * 1024),
+    )(docs)
+
+
+def order_kernel(mine, near_ref, far_ref, out_ref):
+    odd = mine[0] % 2
+    high = mine[0] // 2
+    rows = near_ref.shape[0] // 2
+    near = [near_ref[:rows].astype(F32), near_ref[rows:].astype(F32)]
+    far = [far_ref[:rows].astype(F32), far_ref[rows:].astype(F32)]
+    near = [jnp.where(odd == k, near[0], near[1]) for k in range(2)]
+    far = [jnp.where(odd == k, far[1], far[0]) for k in range(2)]
+    low = [jnp.where(high == 0, near[k], far[k]) for k in range(2)]
+    top = [jnp.where(high == 0, far[k], near[k]) for k in range(2)]
+    out_ref[...] = jnp.concatenate(low + top, axis=0).T
+
+
+def in_order(mine, near, far):
+    rows, n_docs = near.shape
     vmem = pl.BlockSpec(memory_space=pltpu.VMEM)
     return pl.pallas_call(
         order_kernel,
-        in_specs=[pl.BlockSpec(memory_space=pltpu.SMEM)] + [vmem] * len(turn),
+        in_specs=[pl.BlockSpec(memory_space=pltpu.SMEM), vmem, vmem],
         out_specs=vmem,
-        out_shape=jax.ShapeDtypeStruct((n_docs, rows * len(turn)), F32),
+        out_shape=jax.ShapeDtypeStruct((n_docs, 2 * rows), F32),
         compiler_params=pltpu.CompilerParams(vmem_limit_bytes=8 * 1024 * 1024),
-    )(mine.reshape(1).astype(jnp.int32), *turn)
+    )(mine.reshape(1).astype(jnp.int32), near, far)
 
 
 def halves(scores):
@@ -184,8 +201,8 @@
     blocks = first_weight.reshape(1, 4, pair, rows, width)
     blocks = jnp.broadcast_to(blocks, (n_za, *blocks.shape[1:])).reshape(n_za * 4, pair, rows, width)
     along_z = exchange(blocks, ("za", "zp", "core"))
-    docs = embeddings
-    docs_near = swap(docs, "zp")
+    docs = staged(embeddings)
+    docs_near = swap(embeddings, "zp")
     first_a = to_all(along_z, "x")
     first_b = swap(first_a, "core")
     classes = second_weight.shape[2]
@@ -206,10 +223,10 @@
     answer = swap(message, "zh")
     total = message.astype(F32) + answer.astype(F32)
     mean_quarter = (total[:quarter] * (1.0 / members)).astype(BF16)
-    turn = [mean_quarter]
-    for k in range(1, n_y):
-        turn.append(lax.ppermute(mean_quarter, "y", [(i, (i + k) % n_y) for i in range(n_y)]))
-    mean_logits = in_order(lax.axis_index("y"), turn)
+    paired = lax.ppermute(mean_quarter, "y", [(i, i ^ 1) for i in range(n_y)])
+    pair_rows = jnp.concatenate([mean_quarter, paired], axis=0)
+    crossed = lax.ppermute(pair_rows, "y", [(i, n_y - 1 - i) for i in range(n_y)])
+    mean_logits = in_order(lax.axis_index("y"), pair_rows, crossed)
     scores = total[quarter : quarter + members] + total[quarter + members :]
 
     cutoffs = thresholds.astype(F32) / 256.0

time: 191 us -> 195 us (1.021)
  waiting for transfers between devices: 46 us -> 53.6 us
  starting transfers between devices: 37.9 us -> 33.8 us
    all_to_all x2, waiting for transfers between devices: 4.87 us -> 12 us  [exchange(): return lax.all_to_all(blocks, axes, split_axis=0, concat_axis=0, tiled=True)]
    ppermute x3 -> x2, starting transfers between devices: 9.02 us -> 4.87 us  [the longest x1 2.95 us: step(): lax.ppermute(pair_rows, 'y', [(i, n_y - 1 - i) for i in range(n_y)])]
    ppermute x3 -> x2, waiting for transfers between devices: 1.12 us -> 3.09 us  [the longest x1 3.09 us: step(): lax.ppermute(pair_rows, 'y', [(i, n_y - 1 - i) for i in range(n_y)])]
  transfers between devices with their start and end apart: 8 -> 7, of which waited for: 5 -> 5; matrix products, arithmetic and copies ran while one was open for 1% -> 1% of each run, Pallas kernels for 4% -> 5%
where the time goes in v5:
time: 195 us; the launch traced here: 194 us
  blocking collectives  82.3 us (42%)
  waiting for transfers between devices  53.6 us (27%)
  starting transfers between devices  33.8 us (17%)
  Pallas kernels  16.8 us (9%)
  local copies, waits for them, and re-layouts  4.26 us (2%)
    all_to_all x3, blocking collectives, exchange(): return lax.all_to_all(blocks, axes, split_axis=0, concat_axis=0, tiled=True)  82.3 us
    ppermute x3, waiting for transfers between devices, swap(): return lax.ppermute(array, axis, [(0, 1), (1, 0)])  38.5 us
    all_to_all x2, starting transfers between devices, exchange(): return lax.all_to_all(blocks, axes, split_axis=0, concat_axis=0, tiled=True)  15.7 us
    pallas_call x2, Pallas kernels, score(): pl.pallas_call(functools.partial(score_kernel, last), grid_spec=pltpu.Pre...  14.5 us
    ppermute x3, starting transfers between devices, swap(): return lax.ppermute(array, axis, [(0, 1), (1, 0)])  13.2 us
    all_to_all x2, waiting for transfers between devices, exchange(): return lax.all_to_all(blocks, axes, split_axis=0, concat_axis=0, tiled=True)  12 us
  transfers between devices with their start and end apart: 7, of which 5 were waited for; matrix products, arithmetic and copies ran while one was open for 1% of the time, Pallas kernels for 5%

profile of v5, /device:TPU:1, one launch (start us, length us, event | category | flops | bytes accessed | tf_op | source)
XLA Modules:
  0.0 193.5 jit_solution(6550383168977513143)
XLA Ops:
  0.6 1.0 broadcast_in_dim.20
  1.6 40.1 %all_to_all.25 = bf16[16,2,16,512]{3,2,1,0:T(8,128)(2,1)S(1)} all-to-all(bf16[16,2,16,512]{3,2,1,0:T(8,128)(2,1)S(1)} %bitcast.14), channel_id=1, replica_groups=mesh['za'=4,'zp'=2,'x'=4,'core'=2,'y'=4,'zh'=2] {'za','zp','core'}, dimensions={0} | all-to-all | bytes 1048576 | tf_op jit(solution)/shard_map/all_to_all | solution.py:18
  41.6 0.3 broadcast_in_dim.21
  41.9 30.5 %all_to_all.26.first_ref = bf16[4,16,2,16,512]{4,3,2,1,0:T(8,128)(2,1)} all-to-all(bf16[4,16,2,16,512]{4,3,2,1,0:T(8,128)(2,1)S(1)} %broadcast_in_dim.21), channel_id=1, replica_groups=mesh['za'=4,'zp'=2,'x'=4,'core'=2,'y'=4,'zh'=2] {'x'}, dimensions={0} | all-to-all | bytes 4194304 | tf_op jit(solution)/shard_map/all_to_all | solution.py:18
  72.4 0.0 copy-start.2
  72.4 2.7 %collective-permute-start.1 = (bf16[4,16,2,16,512]{4,3,2,1,0:T(8,128)(2,1)}, bf16[4,16,2,16,512]{4,3,2,1,0:T(8,128)(2,1)}, u32[]{:S(2)}, u32[]{:S(2)}) collective-permute-start(bf16[4,16,2,16,512]{4,3,2,1,0:T(8,128)(2,1)} %all_to_all.26.first_ref), channel_id=1, source_target_pairs={{0,8},{8,0},{1,9},{9,1},{2,10},{10,2},{3,11},{11,3},{4,12},{12,4},... | collective-permute-start | bytes 6291464 | tf_op jit(solution)/shard_map/ppermute | solution.py:26
  75.2 2.5 %collective-permute-start = (bf16[768,1024]{1,0:T(8,128)(2,1)}, bf16[768,1024]{1,0:T(8,128)(2,1)S(1)}, u32[]{:S(2)}, u32[]{:S(2)}) collective-permute-start(bf16[768,1024]{1,0:T(8,128)(2,1)} %docs_hbm.1), channel_id=1, source_target_pairs={{0,64},{64,0},{1,65},{65,1},{2,66},{66,2},{3,67},{67,3},{4,68},{68... | collective-permute-start | bytes 4718600 | tf_op jit(solution)/shard_map/ppermute | solution.py:26
  77.7 1.4 shard_map.85.own_docs_ref
  79.2 0.1 add_add_fusion.scalars
  79.2 0.1 add_add_fusion.1.scalars
  79.3 33.9 %collective-permute-done.near_docs_hbm = bf16[768,1024]{1,0:T(8,128)(2,1)S(1)} collective-permute-done((bf16[768,1024]{1,0:T(8,128)(2,1)}, bf16[768,1024]{1,0:T(8,128)(2,1)S(1)}, u32[]{:S(2)}, u32[]{:S(2)}) %collective-permute-start) | collective-permute-done | bytes 1572896 | tf_op jit(solution)/shard_map/ppermute | solution.py:26
  113.2 0.0 copy-done.2
  113.2 0.0 copy-start
  113.2 1.2 copy-done
  114.4 0.0 copy-start.1
  114.4 7.4 %shard_map.86.refs_0_ = f32[2,136,768]{2,1,0:T(8,128)S(1)} custom-call(s32[3]{0:T(128)S(1)} %add_add_fusion.1.scalars, bf16[768,1024]{1,0:T(8,128)(2,1)S(1)} %shard_map.85.own_docs_ref, bf16[768,1024]{1,0:T(8,128)(2,1)S(1)} %collective-permute-done.near_docs_hbm, bf16[4,16,2,16,512]{4,3,2,1,0:T(8,128)(2,1)} %all_to_all.26.first_ref, ...), custom_call_target="tpu_custom_call" | custom-call | tf_op jit(solution)/shard_map/pallas_call | solution.py:124
  121.8 0.0 collective-permute-done.1.first_ref
  121.8 0.0 copy-done.1
  121.8 7.1 %shard_map.87 = bf16[8,40,768]{2,1,0:T(8,128)(2,1)S(1)} custom-call(s32[3]{0:T(128)S(1)} %add_add_fusion.scalars, bf16[768,1024]{1,0:T(8,128)(2,1)S(1)} %shard_map.85.own_docs_ref, bf16[768,1024]{1,0:T(8,128)(2,1)S(1)} %collective-permute-done.near_docs_hbm, bf16[4,16,2,16,512]{4,3,2,1,0:T(8,128)(2,1)} %collective-permute-done.1.first_ref, ...), custom_call_target="tpu_custom_call" | custom-call | tf_op jit(solution)/shard_map/pallas_call | solution.py:124
  128.9 0.0 copy-start.4
  128.9 0.0 copy-start.3
  129.0 11.7 %all_to_all.27 = bf16[8,40,768]{2,1,0:T(8,128)(2,1)S(1)} all-to-all(bf16[8,40,768]{2,1,0:T(8,128)(2,1)S(1)} %shard_map.87), channel_id=1, replica_groups=mesh['za'=4,'zp'=2,'x'=4,'core'=2,'y'=4,'zh'=2] {'zp','y'}, dimensions={0} | all-to-all | bytes 983040 | tf_op jit(solution)/shard_map/all_to_all | solution.py:18
  140.7 0.1 reshape.69
  140.8 0.1 convert_reduce_fusion
  141.0 7.9 %collective-permute-start.2 = (bf16[48,768]{1,0:T(8,128)(2,1)S(1)}, bf16[48,768]{1,0:T(8,128)(2,1)S(1)}, u32[]{:S(2)}, u32[]{:S(2)}) collective-permute-start(bf16[48,768]{1,0:T(8,128)(2,1)S(1)} %pad_maximum_fusion.1), channel_id=1, source_target_pairs={{0,1},{1,0},{2,3},{3,2},{4,5},{5,4},{6,7},{7,6},{8,9},{9,8},{10,11... | collective-permute-start | bytes 221192 | tf_op jit(solution)/shard_map/ppermute | solution.py:26
  148.9 0.0 copy-done.4
  148.9 0.6 fusion.4
  149.5 0.0 copy-done.3
  150.2 4.6 %collective-permute-done.2 = bf16[48,768]{1,0:T(8,128)(2,1)S(1)} collective-permute-done((bf16[48,768]{1,0:T(8,128)(2,1)S(1)}, bf16[48,768]{1,0:T(8,128)(2,1)S(1)}, u32[]{:S(2)}, u32[]{:S(2)}) %collective-permute-start.2) | collective-permute-done | bytes 73760 | tf_op jit(solution)/shard_map/ppermute | solution.py:26
  154.8 0.1 fusion.3
  154.9 0.2 fusion.5
  155.1 0.6 broadcast_in_dim.22
  155.7 7.4 %all-to-all-start.3 = ((f32[8,2,8]{2,1,0:T(2,128)}), f32[8,2,8]{2,1,0:T(2,128)S(1)}, u32[]{:S(2)}, u32[]{:S(2)}) async-start(f32[8,2,8]{2,1,0:T(2,128)} %broadcast_in_dim.22), calls=%async_computation.3 | async-start | bytes 16384 | tf_op jit(solution)/shard_map/all_to_all | solution.py:18
  163.1 4.6 %all-to-all-done.3 = f32[8,2,8]{2,1,0:T(2,128)S(1)} async-done(((f32[8,2,8]{2,1,0:T(2,128)}), f32[8,2,8]{2,1,0:T(2,128)S(1)}, u32[]{:S(2)}, u32[]{:S(2)}) %all-to-all-start.3) | async-done | bytes 544 | tf_op jit(solution)/shard_map/all_to_all | solution.py:18
  167.8 0.6 broadcast_in_dim.23
  168.4 8.3 %all-to-all-start.4 = ((f32[8,2,8]{2,1,0:T(2,128)}), f32[8,2,8]{2,1,0:T(2,128)S(1)}, u32[]{:S(2)}, u32[]{:S(2)}) async-start(f32[8,2,8]{2,1,0:T(2,128)} %broadcast_in_dim.23), calls=%async_computation.4 | async-start | bytes 16384 | tf_op jit(solution)/shard_map/all_to_all | solution.py:18
  176.7 1.9 collective-permute-start.3
  178.6 7.3 %all-to-all-done.4 = f32[8,2,8]{2,1,0:T(2,128)S(1)} async-done(((f32[8,2,8]{2,1,0:T(2,128)}), f32[8,2,8]{2,1,0:T(2,128)S(1)}, u32[]{:S(2)}, u32[]{:S(2)}) %all-to-all-start.4) | async-done | bytes 544 | tf_op jit(solution)/shard_map/all_to_all | solution.py:18
  186.0 0.1 dynamic-slice_multiply_fusion
  186.0 0.0 collective-permute-done.3
  186.1 3.0 %collective-permute-start.4 = (bf16[64,768]{1,0:T(8,128)(2,1)S(1)}, bf16[64,768]{1,0:T(8,128)(2,1)S(1)}, u32[]{:S(2)}, u32[]{:S(2)}) collective-permute-start(bf16[64,768]{1,0:T(8,128)(2,1)S(1)} %pad_maximum_fusion.near_ref), channel_id=1, source_target_pairs={{0,6},{2,4},{4,2},{6,0},{1,7},{3,5},{5,3},{7,1},{8,14},{10,12},{12... | collective-permute-start | bytes 294920 | tf_op jit(solution)/shard_map/ppermute | solution.py:228
  189.0 0.5 fusion.6
  189.5 3.1 %collective-permute-done.4.far_ref = bf16[64,768]{1,0:T(8,128)(2,1)S(1)} collective-permute-done((bf16[64,768]{1,0:T(8,128)(2,1)S(1)}, bf16[64,768]{1,0:T(8,128)(2,1)S(1)}, u32[]{:S(2)}, u32[]{:S(2)}) %collective-permute-start.4) | collective-permute-done | bytes 98336 | tf_op jit(solution)/shard_map/ppermute | solution.py:228
  192.6 0.9 shard_map.88
  (15 shorter events, 0.2 us)
Async XLA Ops:
  72.4 40.8 %copy-start.2 = (bf16[136,128]{1,0:T(8,128)(2,1)S(1)}, bf16[136,128]{1,0:T(8,128)(2,1)}, u32[]{:S(2)}) copy-start(bf16[136,128]{1,0:T(8,128)(2,1)} %constant.47.clone.grades_ref) | copy-start | bytes 104452
  72.4 49.4 %collective-permute-start.1 = (bf16[4,16,2,16,512]{4,3,2,1,0:T(8,128)(2,1)}, bf16[4,16,2,16,512]{4,3,2,1,0:T(8,128)(2,1)}, u32[]{:S(2)}, u32[]{:S(2)}) collective-permute-start(bf16[4,16,2,16,512]{4,3,2,1,0:T(8,128)(2,1)} %all_to_all.26.first_ref), channel_id=1, source_target_pairs={{0,8},{8,0},{1,9},{9,1},{2,10},{10,2},{3,11},{11,3},{4,12},{12,4},... | collective-permute-start | bytes 6291464 | tf_op jit(solution)/shard_map/ppermute | solution.py:26
  75.2 38.0 %collective-permute-start = (bf16[768,1024]{1,0:T(8,128)(2,1)}, bf16[768,1024]{1,0:T(8,128)(2,1)S(1)}, u32[]{:S(2)}, u32[]{:S(2)}) collective-permute-start(bf16[768,1024]{1,0:T(8,128)(2,1)} %docs_hbm.1), channel_id=1, source_target_pairs={{0,64},{64,0},{1,65},{65,1},{2,66},{66,2},{3,67},{67,3},{4,68},{68... | collective-permute-start | bytes 4718600 | tf_op jit(solution)/shard_map/ppermute | solution.py:26
  113.2 1.2 copy-start
  114.4 7.4 %copy-start.1 = (bf16[8,512,128]{2,1,0:T(8,128)(2,1)S(1)}, bf16[8,512,128]{2,1,0:T(8,128)(2,1)}, u32[]{:S(2)}) copy-start(bf16[8,512,128]{2,1,0:T(8,128)(2,1)} %second_ref.3) | copy-start | bytes 3145732
  128.9 19.9 %copy-start.4 = (s32[8]{0:T(128)S(1)}, s32[8]{0:T(128)}, u32[]{:S(2)}) copy-start(s32[8]{0:T(128)} %param.10) | copy-start | bytes 100
  128.9 20.5 %copy-start.3 = (s32[768]{0:T(1024)S(1)}, s32[768]{0:T(1024)}, u32[]{:S(2)}) copy-start(s32[768]{0:T(1024)} %param.7) | copy-start | bytes 9220
  141.0 13.8 %collective-permute-start.2 = (bf16[48,768]{1,0:T(8,128)(2,1)S(1)}, bf16[48,768]{1,0:T(8,128)(2,1)S(1)}, u32[]{:S(2)}, u32[]{:S(2)}) collective-permute-start(bf16[48,768]{1,0:T(8,128)(2,1)S(1)} %pad_maximum_fusion.1), channel_id=1, source_target_pairs={{0,1},{1,0},{2,3},{3,2},{4,5},{5,4},{6,7},{7,6},{8,9},{9,8},{10,11... | collective-permute-start | bytes 221192 | tf_op jit(solution)/shard_map/ppermute | solution.py:26
  155.7 12.1 %all-to-all-start.3 = ((f32[8,2,8]{2,1,0:T(2,128)}), f32[8,2,8]{2,1,0:T(2,128)S(1)}, u32[]{:S(2)}, u32[]{:S(2)}) async-start(f32[8,2,8]{2,1,0:T(2,128)} %broadcast_in_dim.22), calls=%async_computation.3 | async-start | bytes 16384 | tf_op jit(solution)/shard_map/all_to_all | solution.py:18
  168.4 17.6 %all-to-all-start.4 = ((f32[8,2,8]{2,1,0:T(2,128)}), f32[8,2,8]{2,1,0:T(2,128)S(1)}, u32[]{:S(2)}, u32[]{:S(2)}) async-start(f32[8,2,8]{2,1,0:T(2,128)} %broadcast_in_dim.23), calls=%async_computation.4 | async-start | bytes 16384 | tf_op jit(solution)/shard_map/all_to_all | solution.py:18
  176.7 9.4 %collective-permute-start.3 = (bf16[32,768]{1,0:T(8,128)(2,1)S(1)}, bf16[32,768]{1,0:T(8,128)(2,1)S(1)}, u32[]{:S(2)}, u32[]{:S(2)}) collective-permute-start(bf16[32,768]{1,0:T(8,128)(2,1)S(1)} %fusion), channel_id=1, source_target_pairs={{0,2},{2,0},{4,6},{6,4},{1,3},{3,1},{5,7},{7,5},{8,10},{10,8},{12,... | collective-permute-start | bytes 147464 | tf_op jit(solution)/shard_map/ppermute | solution.py:226
  186.1 6.6 %collective-permute-start.4 = (bf16[64,768]{1,0:T(8,128)(2,1)S(1)}, bf16[64,768]{1,0:T(8,128)(2,1)S(1)}, u32[]{:S(2)}, u32[]{:S(2)}) collective-permute-start(bf16[64,768]{1,0:T(8,128)(2,1)S(1)} %pad_maximum_fusion.near_ref), channel_id=1, source_target_pairs={{0,6},{2,4},{4,2},{6,0},{1,7},{3,5},{5,3},{7,1},{8,14},{10,12},{12... | collective-permute-start | bytes 294920 | tf_op jit(solution)/shard_map/ppermute | solution.py:228

commit v6 on v5

--- a/solution.py
+++ b/solution.py
@@ -138,7 +138,7 @@
             scratch_shapes=[pltpu.VMEM(totals, F32)] * last + scratch,
         ),
         out_shape=jax.ShapeDtypeStruct(packed, BF16) if last else jax.ShapeDtypeStruct(totals, F32),
-        compiler_params=pltpu.CompilerParams(dimension_semantics=("arbitrary",), vmem_limit_bytes=14 * 1024 * 1024),
+        compiler_params=pltpu.CompilerParams(dimension_semantics=("arbitrary",), vmem_limit_bytes=22 * 1024 * 1024),
     )(scalars, own_docs, near_docs, first, second, grades, *before)
 
 
@@ -193,7 +193,6 @@
 def step(embeddings, valid_mask, first_weight, second_weight, thresholds):
     members, rows, width = first_weight.shape
     n_docs = embeddings.shape[0]
-    z_axes = ("za", "zp")
     n_za, n_y = lax.axis_size("za"), lax.axis_size("y")
     parity, core = lax.axis_index("zp"), lax.axis_index("core")
     half, pair = members // 2, members // 4
@@ -235,8 +234,8 @@
     ens_score = jnp.sum(scores, axis=0) / members
     ens_kept = jax.nn.sigmoid(4.0 * (ens_score - jnp.mean(cutoffs)))
     counts = jnp.stack([jnp.sum(kept_soft, axis=1), jnp.sum(kept_soft * ens_kept[None, :], axis=1)])
-    counts = to_all(counts, ("x", "core")).sum(axis=0)
-    counts = to_all(counts, z_axes).sum(axis=0)
+    counts = to_all(counts, ("zp", "x", "core")).sum(axis=0)
+    counts = to_all(counts, "za").sum(axis=0)
     member = lax.axis_index("y") * 2 + lax.axis_index("zh")
     shares = lax.dynamic_slice_in_dim(counts, member, 1, 1) / n_docs
     return mean_logits, shares[0], shares[1]

time: 195 us -> 195 us (level)
  no operation moved by 1% of the time
where the time goes in v6:
time: 195 us; the launch traced here: 194 us
  blocking collectives  82.3 us (42%)
  waiting for transfers between devices  53.8 us (28%)
  starting transfers between devices  33.9 us (17%)
  Pallas kernels  16.8 us (9%)
  local copies, waits for them, and re-layouts  4.26 us (2%)
    all_to_all x3, blocking collectives, exchange(): return lax.all_to_all(blocks, axes, split_axis=0, concat_axis=0, tiled=True)  82.3 us
    ppermute x3, waiting for transfers between devices, swap(): return lax.ppermute(array, axis, [(0, 1), (1, 0)])  38.5 us
    all_to_all x2, starting transfers between devices, exchange(): return lax.all_to_all(blocks, axes, split_axis=0, concat_axis=0, tiled=True)  15.8 us
    pallas_call x2, Pallas kernels, score(): pl.pallas_call(functools.partial(score_kernel, last), grid_spec=pltpu.Pre...  14.5 us
    ppermute x3, starting transfers between devices, swap(): return lax.ppermute(array, axis, [(0, 1), (1, 0)])  13.2 us
    all_to_all x2, waiting for transfers between devices, exchange(): return lax.all_to_all(blocks, axes, split_axis=0, concat_axis=0, tiled=True)  12.2 us
  transfers between devices with their start and end apart: 7, of which 5 were waited for; matrix products, arithmetic and copies ran while one was open for 1% of the time, Pallas kernels for 5%

profile of v6, /device:TPU:1, one launch (start us, length us, event | category | flops | bytes accessed | tf_op | source)
XLA Modules:
  0.0 193.9 jit_solution(5587739457053704966)
XLA Ops:
  0.6 1.0 broadcast_in_dim.20
  1.6 40.1 %all_to_all.25 = bf16[16,2,16,512]{3,2,1,0:T(8,128)(2,1)S(1)} all-to-all(bf16[16,2,16,512]{3,2,1,0:T(8,128)(2,1)S(1)} %bitcast.14), channel_id=1, replica_groups=mesh['za'=4,'zp'=2,'x'=4,'core'=2,'y'=4,'zh'=2] {'za','zp','core'}, dimensions={0} | all-to-all | bytes 1048576 | tf_op jit(solution)/shard_map/all_to_all | solution.py:18
  41.6 0.3 broadcast_in_dim.21
  41.9 30.5 %all_to_all.26.first_ref = bf16[4,16,2,16,512]{4,3,2,1,0:T(8,128)(2,1)} all-to-all(bf16[4,16,2,16,512]{4,3,2,1,0:T(8,128)(2,1)S(1)} %broadcast_in_dim.21), channel_id=1, replica_groups=mesh['za'=4,'zp'=2,'x'=4,'core'=2,'y'=4,'zh'=2] {'x'}, dimensions={0} | all-to-all | bytes 4194304 | tf_op jit(solution)/shard_map/all_to_all | solution.py:18
  72.4 0.0 copy-start.2
  72.4 2.7 %collective-permute-start.1 = (bf16[4,16,2,16,512]{4,3,2,1,0:T(8,128)(2,1)}, bf16[4,16,2,16,512]{4,3,2,1,0:T(8,128)(2,1)}, u32[]{:S(2)}, u32[]{:S(2)}) collective-permute-start(bf16[4,16,2,16,512]{4,3,2,1,0:T(8,128)(2,1)} %all_to_all.26.first_ref), channel_id=1, source_target_pairs={{0,8},{8,0},{1,9},{9,1},{2,10},{10,2},{3,11},{11,3},{4,12},{12,4},... | collective-permute-start | bytes 6291464 | tf_op jit(solution)/shard_map/ppermute | solution.py:26
  75.2 2.5 %collective-permute-start = (bf16[768,1024]{1,0:T(8,128)(2,1)}, bf16[768,1024]{1,0:T(8,128)(2,1)S(1)}, u32[]{:S(2)}, u32[]{:S(2)}) collective-permute-start(bf16[768,1024]{1,0:T(8,128)(2,1)} %docs_hbm.1), channel_id=1, source_target_pairs={{0,64},{64,0},{1,65},{65,1},{2,66},{66,2},{3,67},{67,3},{4,68},{68... | collective-permute-start | bytes 4718600 | tf_op jit(solution)/shard_map/ppermute | solution.py:26
  77.7 1.4 shard_map.85.own_docs_ref
  79.2 0.1 add_add_fusion.scalars
  79.2 0.1 add_add_fusion.1.scalars
  79.3 33.9 %collective-permute-done.near_docs_hbm = bf16[768,1024]{1,0:T(8,128)(2,1)S(1)} collective-permute-done((bf16[768,1024]{1,0:T(8,128)(2,1)}, bf16[768,1024]{1,0:T(8,128)(2,1)S(1)}, u32[]{:S(2)}, u32[]{:S(2)}) %collective-permute-start) | collective-permute-done | bytes 1572896 | tf_op jit(solution)/shard_map/ppermute | solution.py:26
  113.2 0.0 copy-done.2
  113.2 0.0 copy-start
  113.2 1.2 copy-done
  114.4 0.0 copy-start.1
  114.4 7.4 %shard_map.86.refs_0_ = f32[2,136,768]{2,1,0:T(8,128)S(1)} custom-call(s32[3]{0:T(128)S(1)} %add_add_fusion.1.scalars, bf16[768,1024]{1,0:T(8,128)(2,1)S(1)} %shard_map.85.own_docs_ref, bf16[768,1024]{1,0:T(8,128)(2,1)S(1)} %collective-permute-done.near_docs_hbm, bf16[4,16,2,16,512]{4,3,2,1,0:T(8,128)(2,1)} %all_to_all.26.first_ref, ...), custom_call_target="tpu_custom_call" | custom-call | tf_op jit(solution)/shard_map/pallas_call | solution.py:124
  121.8 0.0 collective-permute-done.1.first_ref
  121.8 0.0 copy-done.1
  121.8 7.1 %shard_map.87 = bf16[8,40,768]{2,1,0:T(8,128)(2,1)S(1)} custom-call(s32[3]{0:T(128)S(1)} %add_add_fusion.scalars, bf16[768,1024]{1,0:T(8,128)(2,1)S(1)} %shard_map.85.own_docs_ref, bf16[768,1024]{1,0:T(8,128)(2,1)S(1)} %collective-permute-done.near_docs_hbm, bf16[4,16,2,16,512]{4,3,2,1,0:T(8,128)(2,1)} %collective-permute-done.1.first_ref, ...), custom_call_target="tpu_custom_call" | custom-call | tf_op jit(solution)/shard_map/pallas_call | solution.py:124
  128.9 0.0 copy-start.4
  128.9 0.0 copy-start.3
  129.0 11.7 %all_to_all.27 = bf16[8,40,768]{2,1,0:T(8,128)(2,1)S(1)} all-to-all(bf16[8,40,768]{2,1,0:T(8,128)(2,1)S(1)} %shard_map.87), channel_id=1, replica_groups=mesh['za'=4,'zp'=2,'x'=4,'core'=2,'y'=4,'zh'=2] {'zp','y'}, dimensions={0} | all-to-all | bytes 983040 | tf_op jit(solution)/shard_map/all_to_all | solution.py:18
  140.7 0.1 reshape.69
  140.8 0.1 convert_reduce_fusion
  141.0 7.9 %collective-permute-start.2 = (bf16[48,768]{1,0:T(8,128)(2,1)S(1)}, bf16[48,768]{1,0:T(8,128)(2,1)S(1)}, u32[]{:S(2)}, u32[]{:S(2)}) collective-permute-start(bf16[48,768]{1,0:T(8,128)(2,1)S(1)} %pad_maximum_fusion.1), channel_id=1, source_target_pairs={{0,1},{1,0},{2,3},{3,2},{4,5},{5,4},{6,7},{7,6},{8,9},{9,8},{10,11... | collective-permute-start | bytes 221192 | tf_op jit(solution)/shard_map/ppermute | solution.py:26
  148.9 0.0 copy-done.4
  148.9 0.6 fusion.4
  149.5 0.0 copy-done.3
  150.2 4.6 %collective-permute-done.2 = bf16[48,768]{1,0:T(8,128)(2,1)S(1)} collective-permute-done((bf16[48,768]{1,0:T(8,128)(2,1)S(1)}, bf16[48,768]{1,0:T(8,128)(2,1)S(1)}, u32[]{:S(2)}, u32[]{:S(2)}) %collective-permute-start.2) | collective-permute-done | bytes 73760 | tf_op jit(solution)/shard_map/ppermute | solution.py:26
  154.8 0.1 fusion.3
  154.9 0.2 fusion.5
  155.1 0.6 broadcast_in_dim.22
  155.7 8.2 %all-to-all-start.3 = ((f32[16,2,8]{2,1,0:T(2,128)}), f32[16,2,8]{2,1,0:T(2,128)S(1)}, u32[]{:S(2)}, u32[]{:S(2)}) async-start(f32[16,2,8]{2,1,0:T(2,128)} %broadcast_in_dim.22), calls=%async_computation.3 | async-start | bytes 32768 | tf_op jit(solution)/shard_map/all_to_all | solution.py:18
  163.9 5.8 %all-to-all-done.3 = f32[16,2,8]{2,1,0:T(2,128)S(1)} async-done(((f32[16,2,8]{2,1,0:T(2,128)}), f32[16,2,8]{2,1,0:T(2,128)S(1)}, u32[]{:S(2)}, u32[]{:S(2)}) %all-to-all-start.3) | async-done | bytes 1056 | tf_op jit(solution)/shard_map/all_to_all | solution.py:18
  169.7 0.6 broadcast_in_dim.23
  170.3 7.7 %all-to-all-start.4 = ((f32[4,2,8]{2,1,0:T(2,128)}), f32[4,2,8]{2,1,0:T(2,128)S(1)}, u32[]{:S(2)}, u32[]{:S(2)}) async-start(f32[4,2,8]{2,1,0:T(2,128)} %broadcast_in_dim.23), calls=%async_computation.4 | async-start | bytes 8192 | tf_op jit(solution)/shard_map/all_to_all | solution.py:18
  177.9 1.9 collective-permute-start.3
  179.9 6.4 %all-to-all-done.4 = f32[4,2,8]{2,1,0:T(2,128)S(1)} async-done(((f32[4,2,8]{2,1,0:T(2,128)}), f32[4,2,8]{2,1,0:T(2,128)S(1)}, u32[]{:S(2)}, u32[]{:S(2)}) %all-to-all-start.4) | async-done | bytes 288 | tf_op jit(solution)/shard_map/all_to_all | solution.py:18
  186.3 0.1 dynamic-slice_multiply_fusion
  186.4 0.0 collective-permute-done.3
  186.4 3.0 %collective-permute-start.4 = (bf16[64,768]{1,0:T(8,128)(2,1)S(1)}, bf16[64,768]{1,0:T(8,128)(2,1)S(1)}, u32[]{:S(2)}, u32[]{:S(2)}) collective-permute-start(bf16[64,768]{1,0:T(8,128)(2,1)S(1)} %pad_maximum_fusion.near_ref), channel_id=1, source_target_pairs={{0,6},{2,4},{4,2},{6,0},{1,7},{3,5},{5,3},{7,1},{8,14},{10,12},{12... | collective-permute-start | bytes 294920 | tf_op jit(solution)/shard_map/ppermute | solution.py:227
  189.4 0.5 fusion.6
  189.9 3.1 %collective-permute-done.4.far_ref = bf16[64,768]{1,0:T(8,128)(2,1)S(1)} collective-permute-done((bf16[64,768]{1,0:T(8,128)(2,1)S(1)}, bf16[64,768]{1,0:T(8,128)(2,1)S(1)}, u32[]{:S(2)}, u32[]{:S(2)}) %collective-permute-start.4) | collective-permute-done | bytes 98336 | tf_op jit(solution)/shard_map/ppermute | solution.py:227
  193.0 0.9 shard_map.88
  (15 shorter events, 0.2 us)
Async XLA Ops:
  72.4 40.8 %copy-start.2 = (bf16[136,128]{1,0:T(8,128)(2,1)S(1)}, bf16[136,128]{1,0:T(8,128)(2,1)}, u32[]{:S(2)}) copy-start(bf16[136,128]{1,0:T(8,128)(2,1)} %constant.47.clone.grades_ref) | copy-start | bytes 104452
  72.4 49.4 %collective-permute-start.1 = (bf16[4,16,2,16,512]{4,3,2,1,0:T(8,128)(2,1)}, bf16[4,16,2,16,512]{4,3,2,1,0:T(8,128)(2,1)}, u32[]{:S(2)}, u32[]{:S(2)}) collective-permute-start(bf16[4,16,2,16,512]{4,3,2,1,0:T(8,128)(2,1)} %all_to_all.26.first_ref), channel_id=1, source_target_pairs={{0,8},{8,0},{1,9},{9,1},{2,10},{10,2},{3,11},{11,3},{4,12},{12,4},... | collective-permute-start | bytes 6291464 | tf_op jit(solution)/shard_map/ppermute | solution.py:26
  75.2 38.0 %collective-permute-start = (bf16[768,1024]{1,0:T(8,128)(2,1)}, bf16[768,1024]{1,0:T(8,128)(2,1)S(1)}, u32[]{:S(2)}, u32[]{:S(2)}) collective-permute-start(bf16[768,1024]{1,0:T(8,128)(2,1)} %docs_hbm.1), channel_id=1, source_target_pairs={{0,64},{64,0},{1,65},{65,1},{2,66},{66,2},{3,67},{67,3},{4,68},{68... | collective-permute-start | bytes 4718600 | tf_op jit(solution)/shard_map/ppermute | solution.py:26
  113.2 1.2 copy-start
  114.4 7.4 %copy-start.1 = (bf16[8,512,128]{2,1,0:T(8,128)(2,1)S(1)}, bf16[8,512,128]{2,1,0:T(8,128)(2,1)}, u32[]{:S(2)}) copy-start(bf16[8,512,128]{2,1,0:T(8,128)(2,1)} %second_ref.3) | copy-start | bytes 3145732
  128.9 19.9 %copy-start.4 = (s32[8]{0:T(128)S(1)}, s32[8]{0:T(128)}, u32[]{:S(2)}) copy-start(s32[8]{0:T(128)} %param.10) | copy-start | bytes 100
  128.9 20.5 %copy-start.3 = (s32[768]{0:T(1024)S(1)}, s32[768]{0:T(1024)}, u32[]{:S(2)}) copy-start(s32[768]{0:T(1024)} %param.7) | copy-start | bytes 9220
  141.0 13.8 %collective-permute-start.2 = (bf16[48,768]{1,0:T(8,128)(2,1)S(1)}, bf16[48,768]{1,0:T(8,128)(2,1)S(1)}, u32[]{:S(2)}, u32[]{:S(2)}) collective-permute-start(bf16[48,768]{1,0:T(8,128)(2,1)S(1)} %pad_maximum_fusion.1), channel_id=1, source_target_pairs={{0,1},{1,0},{2,3},{3,2},{4,5},{5,4},{6,7},{7,6},{8,9},{9,8},{10,11... | collective-permute-start | bytes 221192 | tf_op jit(solution)/shard_map/ppermute | solution.py:26
  155.7 14.0 %all-to-all-start.3 = ((f32[16,2,8]{2,1,0:T(2,128)}), f32[16,2,8]{2,1,0:T(2,128)S(1)}, u32[]{:S(2)}, u32[]{:S(2)}) async-start(f32[16,2,8]{2,1,0:T(2,128)} %broadcast_in_dim.22), calls=%async_computation.3 | async-start | bytes 32768 | tf_op jit(solution)/shard_map/all_to_all | solution.py:18
  170.3 16.0 %all-to-all-start.4 = ((f32[4,2,8]{2,1,0:T(2,128)}), f32[4,2,8]{2,1,0:T(2,128)S(1)}, u32[]{:S(2)}, u32[]{:S(2)}) async-start(f32[4,2,8]{2,1,0:T(2,128)} %broadcast_in_dim.23), calls=%async_computation.4 | async-start | bytes 8192 | tf_op jit(solution)/shard_map/all_to_all | solution.py:18
  177.9 8.4 %collective-permute-start.3 = (bf16[32,768]{1,0:T(8,128)(2,1)S(1)}, bf16[32,768]{1,0:T(8,128)(2,1)S(1)}, u32[]{:S(2)}, u32[]{:S(2)}) collective-permute-start(bf16[32,768]{1,0:T(8,128)(2,1)S(1)} %fusion), channel_id=1, source_target_pairs={{0,2},{2,0},{4,6},{6,4},{1,3},{3,1},{5,7},{7,5},{8,10},{10,8},{12,... | collective-permute-start | bytes 147464 | tf_op jit(solution)/shard_map/ppermute | solution.py:225
  186.4 6.6 %collective-permute-start.4 = (bf16[64,768]{1,0:T(8,128)(2,1)S(1)}, bf16[64,768]{1,0:T(8,128)(2,1)S(1)}, u32[]{:S(2)}, u32[]{:S(2)}) collective-permute-start(bf16[64,768]{1,0:T(8,128)(2,1)S(1)} %pad_maximum_fusion.near_ref), channel_id=1, source_target_pairs={{0,6},{2,4},{4,2},{6,0},{1,7},{3,5},{5,3},{7,1},{8,14},{10,12},{12... | collective-permute-start | bytes 294920 | tf_op jit(solution)/shard_map/ppermute | solution.py:227
